TPU v7x, 128 devices: a whole 4x4x4 slice. The times are simulated.
128 devices in a mesh: dp: 2 (over z_lo), seq: 64 (over z_hi, y, x, core).
Axes of the slice: x: 4, y: 4, z: 4 (z_hi: 2, z_lo: 2; z = z_hi * 2 + z_lo), core: 2. Of those that a mesh axis runs over, the one named last changes fastest.
Arguments:
- grad_out: bfloat16 [2, 16384, 512], P('dp', 'seq'), may hold values from -6 to 6
- gate: bfloat16 [2, 16384, 512], P('dp', 'seq'), may hold values from -6 to 6
- signal: bfloat16 [2, 16384, 512], P('dp', 'seq'), may hold values from -6 to 6
- filters: float32 [2, 256, 16384], P(None, 'seq', 'dp'), may hold values from -0.046875 to 0.046875
Outputs:
- grad_signal: bfloat16 [2, 16384, 512], P('dp', 'seq')
- grad_gate: bfloat16 [2, 16384, 512], P('dp', 'seq')
- grad_filter: float32 [2, 256, 16384], P(None, 'seq', 'dp')
All inputs are finite; a program needn't handle non-finite values.
Results may differ from a plain program's by a relative error of at most 0.005.
Values may be sent and summed in bfloat16 or wider, within the bound.
A program may use at most 128 MiB of HBM per device.

v0:
```python
import math

import jax
import jax.numpy as jnp
from jax import lax
from jax.sharding import PartitionSpec as P

highest = lax.Precision.HIGHEST


def in_order(pieces, dim):
    dims = list(pieces.shape[1:])
    dims[dim] *= pieces.shape[0]
    return jnp.moveaxis(pieces, 0, dim).reshape(dims)


def sent_to_all(x, axis):
    devices = lax.axis_size(axis)
    return lax.all_to_all(jnp.broadcast_to(x[None], (devices, *x.shape)), axis, 0, 0, tiled=True)


def gathered_copies(x, axis, dim):
    return in_order(sent_to_all(x, axis), dim)


def cut_along(x, dim, devices):
    before, after = (x.shape[:dim], x.shape[dim + 1 :])
    return jnp.moveaxis(x.reshape(*before, devices, -1, *after), dim, 0)


def sent_and_summed(x, axis, dim):
    pieces = cut_along(x, dim, lax.axis_size(axis))
    arrived = lax.all_to_all(pieces, axis, split_axis=0, concat_axis=0, tiled=True)
    return arrived.sum(axis=0)


def split_factor(length):
    columns = length
    while columns * columns > 2 * length and columns % 2 == 0:
        columns = columns // 2
    return columns


def phase_table(height, breadth, period):
    row_index = lax.broadcasted_iota(jnp.int32, (height, breadth), 0)
    column_index = lax.broadcasted_iota(jnp.int32, (height, breadth), 1)
    product_mod = row_index * column_index % period
    angles = product_mod.astype(jnp.float32) * (2.0 * math.pi / period)
    return (jnp.cos(angles), -jnp.sin(angles))


def make_tables(length):
    columns = split_factor(length)
    tile_rows = 2 * length // columns
    outer_table = phase_table(tile_rows, tile_rows, tile_rows)
    inner_table = phase_table(columns, columns, columns)
    twiddle = phase_table(tile_rows, columns, tile_rows * columns)
    return (tile_rows, columns, outer_table, inner_table, twiddle)


def right_product(values, matrix):
    return jnp.einsum("ckq,qm->ckm", values, matrix, precision=highest)


def forward_dft(values, tables):
    tile_rows, columns, outer_table, inner_table, twiddle = tables
    stacked = values.shape[0]
    kept_rows = tile_rows // 2
    blocks = values.astype(jnp.float32).reshape(stacked, kept_rows, columns)
    section_real = jnp.einsum(
        "kh,chq->ckq", outer_table[0][:, :kept_rows], blocks, precision=highest
    )
    section_imaginary = jnp.einsum(
        "kh,chq->ckq", outer_table[1][:, :kept_rows], blocks, precision=highest
    )
    turned_real = section_real * twiddle[0] - section_imaginary * twiddle[1]
    turned_imaginary = section_real * twiddle[1] + section_imaginary * twiddle[0]
    spectrum_real = right_product(turned_real, inner_table[0]) - right_product(
        turned_imaginary, inner_table[1]
    )
    spectrum_imaginary = right_product(turned_real, inner_table[1]) + right_product(
        turned_imaginary, inner_table[0]
    )
    return (spectrum_real, spectrum_imaginary)


def inverse_dft(spectrum_real, spectrum_imaginary, tables):
    tile_rows, columns, outer_table, inner_table, twiddle = tables
    stacked = spectrum_real.shape[0]
    kept_rows = tile_rows // 2
    back_real = right_product(spectrum_real, inner_table[0]) + right_product(
        spectrum_imaginary, inner_table[1]
    )
    back_imaginary = right_product(spectrum_imaginary, inner_table[0]) - right_product(
        spectrum_real, inner_table[1]
    )
    turned_real = back_real * twiddle[0] + back_imaginary * twiddle[1]
    turned_imaginary = back_imaginary * twiddle[0] - back_real * twiddle[1]
    result = jnp.einsum("nk,ckq->cnq", outer_table[0][:kept_rows], turned_real, precision=highest)
    result = result + jnp.einsum(
        "nk,ckq->cnq", outer_table[1][:kept_rows], turned_imaginary, precision=highest
    )
    return result.reshape(stacked, kept_rows * columns) / (tile_rows * columns)


def channel_pass(scaled_rows, signal_rows, filter_real, filter_imaginary, tables):
    scaled_real, scaled_imaginary = forward_dft(scaled_rows, tables)
    signal_real, signal_imaginary = forward_dft(signal_rows, tables)
    convolved = inverse_dft(
        filter_real * signal_real - filter_imaginary * signal_imaginary,
        filter_real * signal_imaginary + filter_imaginary * signal_real,
        tables,
    )
    adjoint = inverse_dft(
        filter_real * scaled_real + filter_imaginary * scaled_imaginary,
        filter_real * scaled_imaginary - filter_imaginary * scaled_real,
        tables,
    )
    kernels = inverse_dft(
        scaled_real * signal_real + scaled_imaginary * signal_imaginary,
        scaled_imaginary * signal_real - scaled_real * signal_imaginary,
        tables,
    )
    return (convolved, adjoint, kernels)


def on_device(grad_out, gate, signal, filters):
    local_rows = grad_out.shape[1]
    pieces = lax.axis_size("seq")
    length = local_rows * pieces
    segments = filters.shape[0]
    per_device = filters.shape[1]
    segment_width = per_device * pieces
    tables = make_tables(length)
    tile_rows, columns = (tables[0], tables[1])
    gradient = grad_out[0].astype(jnp.float32)
    scaled = (gradient * gate[0].astype(jnp.float32)).astype(jnp.bfloat16)
    scaled = scaled.reshape(local_rows, segments, segment_width)
    inputs = signal[0].reshape(local_rows, segments, segment_width)
    complete = gathered_copies(filters, "dp", 2)
    full_real, full_imaginary = forward_dft(complete.reshape(segments * per_device, length), tables)
    layout = (segments, per_device, tile_rows, columns)
    filter_real = full_real.reshape(layout)
    filter_imaginary = full_imaginary.reshape(layout)
    adjoint_parts = []
    conv_parts = []
    kernel_parts = []
    for segment in range(segments):
        moved_gradient, moved_signal = (
            lax.all_to_all(scaled[:, segment], "seq", split_axis=1, concat_axis=0, tiled=True),
            lax.all_to_all(inputs[:, segment], "seq", split_axis=1, concat_axis=0, tiled=True),
        )
        convolved, adjoint, kernel_rows = channel_pass(
            moved_gradient.T,
            moved_signal.T,
            filter_real[segment],
            filter_imaginary[segment],
            tables,
        )
        adjoint_tokens, conv_tokens = (
            lax.all_to_all(
                adjoint.astype(jnp.bfloat16).T, "seq", split_axis=0, concat_axis=1, tiled=True
            ),
            lax.all_to_all(
                convolved.astype(jnp.bfloat16).T, "seq", split_axis=0, concat_axis=1, tiled=True
            ),
        )
        adjoint_parts.append(adjoint_tokens)
        conv_parts.append(conv_tokens)
        kernel_parts.append(kernel_rows)
    grad_signal = jnp.concatenate(adjoint_parts, axis=1)
    conv_out = jnp.concatenate(conv_parts, axis=1)
    kernels = jnp.stack(kernel_parts)
    grad_gate = (gradient * conv_out.astype(jnp.float32)).astype(jnp.bfloat16)
    factor = (lax.axis_size("dp") * length) ** (-0.5)
    grad_filter = sent_and_summed(kernels * factor, "dp", 2)
    return (grad_signal[None], grad_gate[None], grad_filter)


def solution(mesh):
    placed = (
        P("dp", "seq", None),
        P("dp", "seq", None),
        P("dp", "seq", None),
        P(None, "seq", "dp"),
    )
    return jax.shard_map(
        on_device,
        mesh=mesh,
        in_specs=placed,
        out_specs=(P("dp", "seq", None), P("dp", "seq", None), P(None, "seq", "dp")),
        check_vma=False,
    )
```

profile of v0, /device:TPU:1, one launch (start us, length us, event | category | flops | bytes accessed | tf_op | source)
XLA Modules:
  0.0 222.7 jit_solution(4089273984912874189)
XLA Ops:
  2.4 12.4 %all-to-all-start.7 = ((bf16[256,64,4]{0,2,1:T(4,128)(2,1)}), bf16[256,64,4]{0,2,1:T(4,128)(2,1)S(1)}, u32[]{:S(2)}, u32[]{:S(2)}) async-start(bf16[256,64,4]{0,2,1:T(4,128)(2,1)} %all_to_all.138), calls=%async_computation.7 | async-start | bytes 262144 | tf_op jit(solution)/shard_map/all_to_all | solution.py:151
  21.3 3.6 %all-to-all-done.7 = bf16[256,64,4]{0,2,1:T(4,128)(2,1)S(1)} async-done(((bf16[256,64,4]{0,2,1:T(4,128)(2,1)}), bf16[256,64,4]{0,2,1:T(4,128)(2,1)S(1)}, u32[]{:S(2)}, u32[]{:S(2)}) %all-to-all-start.7) | async-done | bytes 131104 | tf_op jit(solution)/shard_map/all_to_all | solution.py:151
  24.9 6.9 %all-to-all-start.5 = ((bf16[256,64,4]{0,2,1:T(4,128)(2,1)}), bf16[256,64,4]{0,2,1:T(4,128)(2,1)S(1)}, u32[]{:S(2)}, u32[]{:S(2)}) async-start(bf16[256,64,4]{0,2,1:T(4,128)(2,1)} %all_to_all.131), calls=%async_computation.5 | async-start | bytes 262144 | tf_op jit(solution)/shard_map/all_to_all | solution.py:151
  35.8 6.0 %all-to-all-done.5 = bf16[256,64,4]{0,2,1:T(4,128)(2,1)S(1)} async-done(((bf16[256,64,4]{0,2,1:T(4,128)(2,1)}), bf16[256,64,4]{0,2,1:T(4,128)(2,1)S(1)}, u32[]{:S(2)}, u32[]{:S(2)}) %all-to-all-start.5) | async-done | bytes 131104 | tf_op jit(solution)/shard_map/all_to_all | solution.py:151
  41.8 4.4 %all-to-all-start.3 = ((bf16[256,64,4]{0,2,1:T(4,128)(2,1)}), bf16[256,64,4]{0,2,1:T(4,128)(2,1)S(1)}, u32[]{:S(2)}, u32[]{:S(2)}) async-start(bf16[256,64,4]{0,2,1:T(4,128)(2,1)} %all_to_all.123), calls=%async_computation.3 | async-start | bytes 262144 | tf_op jit(solution)/shard_map/all_to_all | solution.py:150
  47.0 9.4 %all-to-all-done.3 = bf16[256,64,4]{0,2,1:T(4,128)(2,1)S(1)} async-done(((bf16[256,64,4]{0,2,1:T(4,128)(2,1)}), bf16[256,64,4]{0,2,1:T(4,128)(2,1)S(1)}, u32[]{:S(2)}, u32[]{:S(2)}) %all-to-all-start.3) | async-done | bytes 131104 | tf_op jit(solution)/shard_map/all_to_all | solution.py:150
  56.4 4.8 %all-to-all-start.1 = ((bf16[256,64,4]{0,2,1:T(4,128)(2,1)}), bf16[256,64,4]{0,2,1:T(4,128)(2,1)S(1)}, u32[]{:S(2)}, u32[]{:S(2)}) async-start(bf16[256,64,4]{0,2,1:T(4,128)(2,1)} %all_to_all.115), calls=%async_computation.1 | async-start | bytes 262144 | tf_op jit(solution)/shard_map/all_to_all | solution.py:150
  65.6 2.0 fusion.155
  72.1 4.2 %all-to-all-start = ((f32[2,2,4,8192]{3,2,1,0:T(4,128)}), f32[2,2,4,8192]{3,2,1,0:T(4,128)}, u32[]{:S(2)}, u32[]{:S(2)}) async-start(f32[2,2,4,8192]{3,2,1,0:T(4,128)} %broadcast_in_dim.4), calls=%async_computation | async-start | bytes 1048576 | tf_op jit(solution)/shard_map/all_to_all | solution.py:19
  83.2 2.0 convolution_subtract_fusion.8
  88.4 2.0 convolution_subtract_fusion.10
  95.1 2.1 fusion.137
  97.3 9.8 %fusion.136 = f32[256,8,128]{2,0,1:T(8,128)S(1)} fusion(f32[8,128,128]{2,1,0:T(8,128)S(1)} %copy-done.17, f32[256,256]{1,0:T(8,128)S(1)} %copy-done.9), kind=kOutput, calls=%fused_computation.213 | convolution fusion | flops 402653184 | bytes 1703936 | tf_op jit(solution)/shard_map/kh,chq->ckq/dot_general | solution.py:70
  113.1 2.7 %multiply_subtract_fusion.5 = (f32[4,256,128]{2,1,0:T(8,128)}, f32[4,256,128]{2,1,0:T(8,128)}, f32[4,256,128]{2,1,0:T(8,128)}, f32[4,256,128]{2,1,0:T(8,128)}, f...) fusion(f32[4,256,128]{2,1,0:T(8,128)S(1)} %copy-done.16, ...), kind=kOutput, calls=%fused_computation.111 | convolution fusion | flops 205225984 | bytes 11272192 | tf_op jit(solution)/shard_map/ckq,qm->ckm/dot_general | solution.py:62
  121.4 10.8 %all-to-all-start.4 = ((bf16[64,256,4]{1,2,0:T(4,128)(2,1)}), bf16[64,256,4]{1,2,0:T(4,128)(2,1)}, u32[]{:S(2)}, u32[]{:S(2)}) async-start(bf16[64,256,4]{1,2,0:T(4,128)(2,1)} %bitcast.26), calls=%async_computation.4 | async-start | bytes 262144 | tf_op jit(solution)/shard_map/all_to_all | solution.py:161
  132.2 3.1 %multiply_add_fusion.2 = (f32[4,256,128]{2,1,0:T(8,128)S(1)}, f32[4,256,128]{2,1,0:T(8,128)S(1)}, f32[4,256,128]{2,1,0:T(8,128)S(1)}, f32[4,256,128]{2,1,0:T(8,128)S(1)}) fusion(f32[4,256,128]{2,1,0:T(8,128)} %get-tuple-element.33, f32[4,256,128]{2,1,0:T(8,128)} %convolution_subtract_fusion.10, f32[4,256,128]{2,1,0:T(8,128)} %convolution_subtract_fusion.6, ...), kind=kOutput, calls=%fused_computation.91 | convolution fusion | flops 203653120 | bytes 6553600 | tf_op jit(solution)/shard_map/ckq,qm->ckm/dot_general | solution.py:62
  160.6 10.7 %all-to-all-start.2 = ((bf16[64,256,4]{1,2,0:T(4,128)(2,1)}), bf16[64,256,4]{1,2,0:T(4,128)(2,1)S(1)}, u32[]{:S(2)}, u32[]{:S(2)}) async-start(bf16[64,256,4]{1,2,0:T(4,128)(2,1)} %bitcast.17), calls=%async_computation.2 | async-start | bytes 262144 | tf_op jit(solution)/shard_map/all_to_all | solution.py:161
  172.9 8.4 %all-to-all-done.2 = bf16[64,256,4]{1,2,0:T(4,128)(2,1)S(1)} async-done(((bf16[64,256,4]{1,2,0:T(4,128)(2,1)}), bf16[64,256,4]{1,2,0:T(4,128)(2,1)S(1)}, u32[]{:S(2)}, u32[]{:S(2)}) %all-to-all-start.2) | async-done | bytes 131104 | tf_op jit(solution)/shard_map/all_to_all | solution.py:161
  181.3 4.4 %all-to-all-start.8 = ((bf16[64,256,4]{1,2,0:T(4,128)(2,1)}), bf16[64,256,4]{1,2,0:T(4,128)(2,1)S(1)}, u32[]{:S(2)}, u32[]{:S(2)}) async-start(bf16[64,256,4]{1,2,0:T(4,128)(2,1)} %bitcast.45), calls=%async_computation.8 | async-start | bytes 262144 | tf_op jit(solution)/shard_map/all_to_all | solution.py:164
  187.8 8.1 %all-to-all-done.8 = bf16[64,256,4]{1,2,0:T(4,128)(2,1)S(1)} async-done(((bf16[64,256,4]{1,2,0:T(4,128)(2,1)}), bf16[64,256,4]{1,2,0:T(4,128)(2,1)S(1)}, u32[]{:S(2)}, u32[]{:S(2)}) %all-to-all-start.8) | async-done | bytes 131104 | tf_op jit(solution)/shard_map/all_to_all | solution.py:164
  195.9 4.4 %all-to-all-start.6 = ((bf16[64,256,4]{1,2,0:T(4,128)(2,1)}), bf16[64,256,4]{1,2,0:T(4,128)(2,1)S(1)}, u32[]{:S(2)}, u32[]{:S(2)}) async-start(bf16[64,256,4]{1,2,0:T(4,128)(2,1)} %bitcast.36), calls=%async_computation.6 | async-start | bytes 262144 | tf_op jit(solution)/shard_map/all_to_all | solution.py:164
  202.8 7.6 %all-to-all-done.6 = bf16[64,256,4]{1,2,0:T(4,128)(2,1)S(1)} async-done(((bf16[64,256,4]{1,2,0:T(4,128)(2,1)}), bf16[64,256,4]{1,2,0:T(4,128)(2,1)S(1)}, u32[]{:S(2)}, u32[]{:S(2)}) %all-to-all-start.6) | async-done | bytes 131104 | tf_op jit(solution)/shard_map/all_to_all | solution.py:164
  210.5 3.5 %all-to-all-start.9 = ((f32[2,2,4,8192]{3,2,1,0:T(4,128)}), f32[2,2,4,8192]{3,2,1,0:T(4,128)S(1)}, u32[]{:S(2)}, u32[]{:S(2)}) async-start(f32[2,2,4,8192]{3,2,1,0:T(4,128)} %copy.150), calls=%async_computation.9 | async-start | bytes 1048576 | tf_op jit(solution)/shard_map/all_to_all | solution.py:33
  216.7 4.9 %all-to-all-done.9 = f32[2,2,4,8192]{3,2,1,0:T(4,128)S(1)} async-done(((f32[2,2,4,8192]{3,2,1,0:T(4,128)}), f32[2,2,4,8192]{3,2,1,0:T(4,128)S(1)}, u32[]{:S(2)}, u32[]{:S(2)}) %all-to-all-start.9) | async-done | bytes 524320 | tf_op jit(solution)/shard_map/all_to_all | solution.py:33
  (177 shorter events, 82.6 us)
Async XLA Ops:
  2.4 13.4 %copy-start.35 = (bf16[1,256,512]{2,1,0:T(8,128)(2,1)S(1)}, bf16[1,256,512]{2,1,0:T(8,128)(2,1)}, u32[]{:S(2)}) copy-start(bf16[1,256,512]{2,1,0:T(8,128)(2,1)} %param.4) | copy-start | bytes 786436
  2.4 22.5 %all-to-all-start.7 = ((bf16[256,64,4]{0,2,1:T(4,128)(2,1)}), bf16[256,64,4]{0,2,1:T(4,128)(2,1)S(1)}, u32[]{:S(2)}, u32[]{:S(2)}) async-start(bf16[256,64,4]{0,2,1:T(4,128)(2,1)} %all_to_all.138), calls=%async_computation.7 | async-start | bytes 262144 | tf_op jit(solution)/shard_map/all_to_all | solution.py:151
  21.3 25.3 %copy-start.6 = (f32[256,256]{1,0:T(8,128)}, f32[256,256]{1,0:T(8,128)S(1)}, u32[]{:S(2)}) copy-start(f32[256,256]{1,0:T(8,128)S(1)} %fusion.126) | copy-start | bytes 786436
  24.9 16.9 %all-to-all-start.5 = ((bf16[256,64,4]{0,2,1:T(4,128)(2,1)}), bf16[256,64,4]{0,2,1:T(4,128)(2,1)S(1)}, u32[]{:S(2)}, u32[]{:S(2)}) async-start(bf16[256,64,4]{0,2,1:T(4,128)(2,1)} %all_to_all.131), calls=%async_computation.5 | async-start | bytes 262144 | tf_op jit(solution)/shard_map/all_to_all | solution.py:151
  41.8 14.6 %all-to-all-start.3 = ((bf16[256,64,4]{0,2,1:T(4,128)(2,1)}), bf16[256,64,4]{0,2,1:T(4,128)(2,1)S(1)}, u32[]{:S(2)}, u32[]{:S(2)}) async-start(bf16[256,64,4]{0,2,1:T(4,128)(2,1)} %all_to_all.123), calls=%async_computation.3 | async-start | bytes 262144 | tf_op jit(solution)/shard_map/all_to_all | solution.py:150
  56.4 4.8 %copy-start.32 = (bf16[256,64,4]{0,2,1:T(4,128)(2,1)}, bf16[256,64,4]{0,2,1:T(4,128)(2,1)S(1)}, u32[]{:S(2)}) copy-start(bf16[256,64,4]{0,2,1:T(4,128)(2,1)S(1)} %all-to-all-done.3) | copy-start | bytes 393220
  56.4 14.8 %all-to-all-start.1 = ((bf16[256,64,4]{0,2,1:T(4,128)(2,1)}), bf16[256,64,4]{0,2,1:T(4,128)(2,1)S(1)}, u32[]{:S(2)}, u32[]{:S(2)}) async-start(bf16[256,64,4]{0,2,1:T(4,128)(2,1)} %all_to_all.115), calls=%async_computation.1 | async-start | bytes 262144 | tf_op jit(solution)/shard_map/all_to_all | solution.py:150
  62.1 3.5 %copy-start.2 = (f32[4,256,128]{1,2,0:T(8,128)}, f32[4,256,128]{1,2,0:T(8,128)S(1)}, u32[]{:S(2)}) copy-start(f32[4,256,128]{1,2,0:T(8,128)S(1)} %convolution_bitcast_fusion) | copy-start | bytes 1572868
  63.6 2.0 copy-start.4
  69.2 2.0 copy-start.34
  72.1 20.4 %all-to-all-start = ((f32[2,2,4,8192]{3,2,1,0:T(4,128)}), f32[2,2,4,8192]{3,2,1,0:T(4,128)}, u32[]{:S(2)}, u32[]{:S(2)}) async-start(f32[2,2,4,8192]{3,2,1,0:T(4,128)} %broadcast_in_dim.4), calls=%async_computation | async-start | bytes 1048576 | tf_op jit(solution)/shard_map/all_to_all | solution.py:19
  83.2 2.0 copy-start.29
  95.1 2.1 copy-start.9
  95.1 2.1 copy-start.17
  110.8 5.0 %copy-start.18 = (f32[8,256,128]{2,1,0:T(8,128)}, f32[8,256,128]{2,1,0:T(8,128)S(1)}, u32[]{:S(2)}) copy-start(f32[8,256,128]{2,1,0:T(8,128)S(1)} %convolution_add_fusion) | copy-start | bytes 3145732
  110.9 1.9 copy-start.25
  110.9 2.0 copy-start.27
  110.9 2.2 copy-start.28
  113.1 2.8 %copy-start.19 = (f32[8,256,128]{2,1,0:T(8,128)}, f32[8,256,128]{2,1,0:T(8,128)S(1)}, u32[]{:S(2)}) copy-start(f32[8,256,128]{2,1,0:T(8,128)S(1)} %convolution_subtract_fusion) | copy-start | bytes 3145732
  121.4 39.2 %all-to-all-start.4 = ((bf16[64,256,4]{1,2,0:T(4,128)(2,1)}), bf16[64,256,4]{1,2,0:T(4,128)(2,1)}, u32[]{:S(2)}, u32[]{:S(2)}) async-start(bf16[64,256,4]{1,2,0:T(4,128)(2,1)} %bitcast.26), calls=%async_computation.4 | async-start | bytes 262144 | tf_op jit(solution)/shard_map/all_to_all | solution.py:161
  160.6 20.6 %all-to-all-start.2 = ((bf16[64,256,4]{1,2,0:T(4,128)(2,1)}), bf16[64,256,4]{1,2,0:T(4,128)(2,1)S(1)}, u32[]{:S(2)}, u32[]{:S(2)}) async-start(bf16[64,256,4]{1,2,0:T(4,128)(2,1)} %bitcast.17), calls=%async_computation.2 | async-start | bytes 262144 | tf_op jit(solution)/shard_map/all_to_all | solution.py:161
  181.3 14.6 %all-to-all-start.8 = ((bf16[64,256,4]{1,2,0:T(4,128)(2,1)}), bf16[64,256,4]{1,2,0:T(4,128)(2,1)S(1)}, u32[]{:S(2)}, u32[]{:S(2)}) async-start(bf16[64,256,4]{1,2,0:T(4,128)(2,1)} %bitcast.45), calls=%async_computation.8 | async-start | bytes 262144 | tf_op jit(solution)/shard_map/all_to_all | solution.py:164
  195.9 14.6 %all-to-all-start.6 = ((bf16[64,256,4]{1,2,0:T(4,128)(2,1)}), bf16[64,256,4]{1,2,0:T(4,128)(2,1)S(1)}, u32[]{:S(2)}, u32[]{:S(2)}) async-start(bf16[64,256,4]{1,2,0:T(4,128)(2,1)} %bitcast.36), calls=%async_computation.6 | async-start | bytes 262144 | tf_op jit(solution)/shard_map/all_to_all | solution.py:164
  210.5 11.2 %all-to-all-start.9 = ((f32[2,2,4,8192]{3,2,1,0:T(4,128)}), f32[2,2,4,8192]{3,2,1,0:T(4,128)S(1)}, u32[]{:S(2)}, u32[]{:S(2)}) async-start(f32[2,2,4,8192]{3,2,1,0:T(4,128)} %copy.150), calls=%async_computation.9 | async-start | bytes 1048576 | tf_op jit(solution)/shard_map/all_to_all | solution.py:33
  (23 other events, 29.1 us)
where the time goes:
time: 227 us; the launch traced here: 223 us
  matrix products  80.4 us (35%)
  starting transfers between devices  66.6 us (29%)
  waiting for transfers between devices  48.4 us (21%)
  local copies, waits for them, and re-layouts  21.8 us (10%)
  other arithmetic  3.87 us (2%)
    dot_general x44, matrix products, right_product(): return jnp.einsum('ckq,qm->ckm', values, matrix, precision=highest)  56.6 us
    all_to_all x2, starting transfers between devices, on_device(): lax.all_to_all(adjoint.astype(jnp.bfloat16).T, 'seq', split_axis=0, conca...  21.5 us
    all_to_all x2, starting transfers between devices, on_device(): lax.all_to_all(inputs[:, segment], 'seq', split_axis=1, concat_axis=0, ti...  19.3 us
    all_to_all x2, waiting for transfers between devices, on_device(): lax.all_to_all(convolved.astype(jnp.bfloat16).T, 'seq', split_axis=0, con...  15.7 us
    dot_general x5, matrix products, forward_dft(): jnp.einsum('kh,chq->ckq', outer_table[0][:, :kept_rows], blocks, precisio...  12.4 us
    unnamed x82, local copies, waits for them, and re-layouts  10.9 us
    all_to_all x2, waiting for transfers between devices, on_device(): lax.all_to_all(scaled[:, segment], 'seq', split_axis=1, concat_axis=0, ti...  9.74 us
    all_to_all x2, waiting for transfers between devices, on_device(): lax.all_to_all(inputs[:, segment], 'seq', split_axis=1, concat_axis=0, ti...  9.59 us
  transfers between devices with their start and end apart: 10, of which 8 were waited for; matrix products, arithmetic and copies ran while one was open for 29% of the time, Pallas kernels for 0%

commit v1 on v0

v1 whole, which is shorter than its diff:
```python
import functools
import math

import jax
import jax.numpy as jnp
import numpy as np
from jax import lax
from jax.experimental import pallas as pl
from jax.experimental.pallas import tpu as pltpu
from jax.sharding import PartitionSpec as P

MESH = pl.DeviceIdType.MESH
bf16 = jnp.bfloat16
f32 = jnp.float32

U = 256
HALF = U // 2


def split_table(table):
    high = jnp.asarray(table, f32).astype(bf16)
    low = (jnp.asarray(table, f32) - high.astype(f32)).astype(bf16)
    return high, low


def np_bf16(table):
    import ml_dtypes

    return np.asarray(table, np.float32).astype(ml_dtypes.bfloat16)


def np_split(table):
    high = np_bf16(table)
    low = np_bf16(np.asarray(table, np.float64) - high.astype(np.float64))
    return high, low


@functools.lru_cache(None)
def make_tables(rows):
    points = 2 * rows * U
    k1 = np.arange(rows)[:, None]
    i = np.arange(rows)[None, :]
    angle = 2 * np.pi * (i * (2 * k1 + 1) % (4 * rows)) / (4 * rows)
    outer = np.concatenate([np.cos(angle), -np.sin(angle)], 0)
    high, low = np_split(outer)
    forward = np.concatenate([high, low, high], 1)
    back_high, back_low = np_split(outer.T * (2.0 / points))
    back = np.concatenate([back_high, back_low, back_high], 1)
    u = np.arange(U)[None, :]
    turn = 2 * np.pi * (u * (2 * k1 + 1)) / (2 * points)
    twiddle = np.stack([np.cos(turn), -np.sin(turn)]).astype(np.float32)
    u0 = np.arange(HALF)[:, None]
    m = np.arange(HALF)[None, :]
    inner = []
    for p in range(2):
        a = 2 * np.pi * (u0 * (2 * m + p) % U) / U
        c, s = np.cos(a), np.sin(a)
        inner.append(np.block([[c, -s], [s, c]]))
    inner = np.stack(inner)
    inner_tables = np.stack(np_split(inner), 1)
    inverse_tables = np.stack(np_split(np.swapaxes(inner, 1, 2)), 1)
    return forward, back, twiddle, inner_tables, inverse_tables


@functools.lru_cache(None)
def make_permutation(pieces, segments, per_device):
    channels = pieces * segments * per_device
    table = np.zeros((channels, channels), np.float32)
    for j in range(pieces):
        for s in range(segments):
            for c in range(per_device):
                row = (j * segments + s) * per_device + c
                table[row, s * pieces * per_device + j * per_device + c] = 1
    return np_bf16(table)


def dot(a, b, dims=((1,), (0,))):
    return lax.dot_general(a, b, (dims, ((), ())), preferred_element_type=f32)


def split(x):
    high = x.astype(bf16)
    return high, (x - high.astype(f32)).astype(bf16)


def pack_kernel(grad_ref, gate_ref, signal_ref, filters_ref, perm_ref, pack_ref, pf_ref):
    pieces = pack_ref.shape[0]
    group = pf_ref.shape[1]
    per_device = filters_ref.shape[1]
    scaled = (grad_ref[...].astype(f32) * gate_ref[...].astype(f32)).astype(bf16)
    parts = []
    for x in (scaled, signal_ref[...]):
        rows = dot(perm_ref[...], x, ((1,), (1,)))
        parts.append(rows.reshape(pieces, group, x.shape[0]))
    pack_ref[...] = jnp.concatenate(parts, 1).astype(bf16)
    for s in range(filters_ref.shape[0]):
        for i in range(pf_ref.shape[0]):
            pf_ref[i, s * per_device : (s + 1) * per_device, :] = filters_ref[
                s, :, i * U : (i + 1) * U
            ]


def start_exchange(src_ref, dst_ref, send_sem, recv_sem):
    me = lax.axis_index("seq")
    pieces = src_ref.shape[0]

    def step(d, carry):
        peer = lax.rem(me + d, pieces)
        pltpu.make_async_remote_copy(
            src_ref=src_ref.at[peer],
            dst_ref=dst_ref.at[me],
            send_sem=send_sem,
            recv_sem=recv_sem,
            device_id={"seq": peer},
            device_id_type=MESH,
        ).start()
        return carry

    lax.fori_loop(1, pieces, step, 0)
    dst_ref[me] = src_ref[me]


def wait_exchange(src_ref, dst_ref, send_sem, recv_sem):
    pieces = src_ref.shape[0]
    whole = pltpu.make_async_remote_copy(
        src_ref=src_ref.at[pl.ds(0, pieces - 1)],
        dst_ref=dst_ref.at[pl.ds(0, pieces - 1)],
        send_sem=send_sem,
        recv_sem=recv_sem,
        device_id={"seq": lax.axis_index("seq")},
        device_id_type=MESH,
    )
    whole.wait_send()
    whole.wait_recv()


def meet(pieces):
    me = lax.axis_index("seq")
    other = 1 - lax.axis_index("dp")
    barrier = pltpu.get_barrier_semaphore()

    def greet(d, carry):
        pl.semaphore_signal(
            barrier, inc=1, device_id={"seq": lax.rem(me + d, pieces)}, device_id_type=MESH
        )
        return carry

    lax.fori_loop(1, pieces, greet, 0)
    pl.semaphore_signal(barrier, inc=1, device_id={"dp": other}, device_id_type=MESH)
    pl.semaphore_wait(barrier, pieces)


def scatter_kernel(pack_ref, pf_ref, recv_ref, filt_ref, send_sem, recv_sem, fsend, frecv):
    pieces = pack_ref.shape[0]
    half = pf_ref.shape[0]
    dp = lax.axis_index("dp")
    meet(pieces)
    mine = filt_ref.at[pl.ds(dp * half, half)]
    copy = pltpu.make_async_remote_copy(
        src_ref=pf_ref,
        dst_ref=mine,
        send_sem=fsend,
        recv_sem=frecv,
        device_id={"dp": 1 - dp},
        device_id_type=MESH,
    )
    copy.start()
    start_exchange(pack_ref, recv_ref, send_sem, recv_sem)
    mine[...] = pf_ref[...]
    copy.wait()
    wait_exchange(pack_ref, recv_ref, send_sem, recv_sem)


def gather_kernel(back_ref, ker_ref, rec_ref, ksum_ref, kbuf, send_sem, recv_sem, ksend, krecv):
    pieces = back_ref.shape[0]
    half = ksum_ref.shape[0]
    dp = lax.axis_index("dp")
    meet(pieces)
    copy = pltpu.make_async_remote_copy(
        src_ref=ker_ref.at[pl.ds((1 - dp) * half, half)],
        dst_ref=kbuf,
        send_sem=ksend,
        recv_sem=krecv,
        device_id={"dp": 1 - dp},
        device_id_type=MESH,
    )
    copy.start()
    start_exchange(back_ref, rec_ref, send_sem, recv_sem)
    copy.wait()
    ksum_ref[...] = ker_ref[pl.ds(dp * half, half)] + kbuf[...]
    wait_exchange(back_ref, rec_ref, send_sem, recv_sem)


def unpack_kernel(factor, rec_ref, ksum_ref, grad_ref, perm_ref, gs_ref, gg_ref, gf_ref):
    pieces, both, tokens = rec_ref.shape
    group = both // 2
    per_device = gf_ref.shape[1]
    rec = rec_ref[...].astype(f32)
    adjoint = rec[:, :group].reshape(pieces * group, tokens).astype(bf16)
    conv = rec[:, group:].reshape(pieces * group, tokens).astype(bf16)
    gs_ref[...] = dot(adjoint, perm_ref[...], ((0,), (0,))).astype(bf16)
    conv_tokens = dot(conv, perm_ref[...], ((0,), (0,)))
    gg_ref[...] = (grad_ref[...].astype(f32) * conv_tokens).astype(bf16)
    for s in range(gf_ref.shape[0]):
        for i in range(ksum_ref.shape[0]):
            gf_ref[s, :, i * U : (i + 1) * U] = (
                ksum_ref[i, s * per_device : (s + 1) * per_device, :] * factor
            )


def spectral_kernel(
    recv_ref, filt_ref, fwd_ref, back_ref, tw_ref, in_ref, inv_ref, out_ref, ker_ref, xs, fs, ys, ks
):
    rows, both, _ = recv_ref.shape
    group = both // 2
    for h in range(2):
        lanes = slice(h * HALF, (h + 1) * HALF)
        xs[h] = recv_ref[:, :, lanes].astype(f32).reshape(rows * both, HALF)
        fs[h] = filt_ref[:, lanes]

    def take(ref, c, count):
        return jnp.concatenate([ref[h, pl.ds(c, rows, stride=count), :] for h in range(2)], 1)

    def put(ref, c, count, value):
        for h in range(2):
            ref[h, pl.ds(c, rows, stride=count), :] = value[:, h * HALF : (h + 1) * HALF]

    def forward(p):
        pr, pi = p[:rows], p[rows:]
        tr, ti = tw_ref[0], tw_ref[1]
        qr = pr * tr - pi * ti
        qi = pr * ti + pi * tr
        a = jnp.concatenate([qr[:, :HALF], qi[:, :HALF]], 1)
        b = jnp.concatenate([qr[:, HALF:], qi[:, HALF:]], 1)
        return a + b, a - b

    def three(x, table_ref, p):
        high, low = split(x)
        return (
            dot(high, table_ref[p, 0]) + dot(low, table_ref[p, 0]) + dot(high, table_ref[p, 1])
        )

    def body(c, carry):
        g = take(xs, c, both).astype(bf16)
        s = take(xs, c + group, both).astype(bf16)
        fh, fl = split(take(fs, c, group))
        short = fwd_ref[:, : 2 * rows]
        stages = [
            dot(fwd_ref[...], jnp.concatenate([fh, fh, fl], 0)),
            dot(short, jnp.concatenate([g, g], 0)),
            dot(short, jnp.concatenate([s, s], 0)),
        ]
        turned = [forward(p) for p in stages]
        parts = []
        for p in range(2):
            spec = three(jnp.concatenate([t[p] for t in turned], 0), in_ref, p)
            fr, fi = spec[:rows, :HALF], spec[:rows, HALF:]
            gr, gi = spec[rows : 2 * rows, :HALF], spec[rows : 2 * rows, HALF:]
            sr, si = spec[2 * rows :, :HALF], spec[2 * rows :, HALF:]
            adj = jnp.concatenate([fr * gr + fi * gi, fr * gi - fi * gr], 1)
            conv = jnp.concatenate([fr * sr - fi * si, fr * si + fi * sr], 1)
            ker = jnp.concatenate([gr * sr + gi * si, gi * sr - gr * si], 1)
            parts.append(three(jnp.concatenate([adj, conv, ker], 0), inv_ref, p))
        plus, minus = parts[0] + parts[1], parts[0] - parts[1]
        tr, ti = tw_ref[0], tw_ref[1]
        results = []
        for n in range(3):
            here = slice(n * rows, (n + 1) * rows)
            zr = jnp.concatenate([plus[here, :HALF], minus[here, :HALF]], 1)
            zi = jnp.concatenate([plus[here, HALF:], minus[here, HALF:]], 1)
            z = jnp.concatenate([zr * tr + zi * ti, zi * tr - zr * ti], 0)
            high, low = split(z)
            results.append(dot(back_ref[...], jnp.concatenate([high, high, low], 0)))
        put(ys, c, both, results[0])
        put(ys, c + group, both, results[1])
        put(ks, c, group, results[2])
        return carry

    lax.fori_loop(0, group, body, 0, unroll=UNROLL)
    for h in range(2):
        lanes = slice(h * HALF, (h + 1) * HALF)
        out_ref[:, :, lanes] = ys[h].reshape(rows, both, HALF).astype(bf16)
        ker_ref[:, lanes] = ks[h]


UNROLL = 2


def vmem(count):
    return [pl.BlockSpec(memory_space=pltpu.VMEM)] * count


def spectral(recv, filt, tables):
    rows, both, _ = recv.shape
    group = both // 2
    out, ker = pl.pallas_call(
        spectral_kernel,
        out_shape=(
            jax.ShapeDtypeStruct(recv.shape, bf16),
            jax.ShapeDtypeStruct((rows * group, U), f32),
        ),
        in_specs=vmem(7),
        out_specs=tuple(vmem(2)),
        scratch_shapes=[
            pltpu.VMEM((2, rows * both, HALF), f32),
            pltpu.VMEM((2, rows * group, HALF), f32),
            pltpu.VMEM((2, rows * both, HALF), f32),
            pltpu.VMEM((2, rows * group, HALF), f32),
        ],
        name="spectral",
    )(recv, filt.reshape(rows * group, U), *tables)
    return out, ker.reshape(rows, group, U)


def on_device(grad_out, gate, signal, filters):
    tokens, channels = grad_out.shape[1:]
    pieces = lax.axis_size("seq")
    halves = lax.axis_size("dp")
    segments, per_device, part = filters.shape
    group = segments * per_device
    rows = part * halves // U
    half = part // U
    tables = [jnp.asarray(t) for t in make_tables(rows)]
    perm = jnp.asarray(make_permutation(pieces, segments, per_device))
    gradient = grad_out[0]
    pack, pf = pl.pallas_call(
        pack_kernel,
        out_shape=(
            jax.ShapeDtypeStruct((pieces, 2 * group, tokens), bf16),
            jax.ShapeDtypeStruct((half, group, U), f32),
        ),
        in_specs=vmem(5),
        out_specs=tuple(vmem(2)),
        name="pack",
    )(gradient, gate[0], signal[0], filters, perm)
    dma = pltpu.SemaphoreType.DMA
    recv, filt = pl.pallas_call(
        scatter_kernel,
        out_shape=(
            jax.ShapeDtypeStruct((pieces, 2 * group, tokens), bf16),
            jax.ShapeDtypeStruct((rows, group, U), f32),
        ),
        in_specs=vmem(2),
        out_specs=tuple(vmem(2)),
        scratch_shapes=[dma, dma, dma, dma],
        compiler_params=pltpu.CompilerParams(collective_id=0, has_side_effects=True),
        name="scatter",
    )(pack, pf)
    back, ker = spectral(recv, filt, tables)
    rec, ksum = pl.pallas_call(
        gather_kernel,
        out_shape=(
            jax.ShapeDtypeStruct((pieces, 2 * group, tokens), bf16),
            jax.ShapeDtypeStruct((half, group, U), f32),
        ),
        in_specs=vmem(2),
        out_specs=tuple(vmem(2)),
        scratch_shapes=[pltpu.VMEM((half, group, U), f32), dma, dma, dma, dma],
        compiler_params=pltpu.CompilerParams(collective_id=1, has_side_effects=True),
        name="gather",
    )(back, ker)
    factor = (halves * rows * U) ** (-0.5)
    grad_signal, grad_gate, grad_filter = pl.pallas_call(
        functools.partial(unpack_kernel, factor),
        out_shape=(
            jax.ShapeDtypeStruct((tokens, channels), bf16),
            jax.ShapeDtypeStruct((tokens, channels), bf16),
            jax.ShapeDtypeStruct((segments, per_device, part), f32),
        ),
        in_specs=vmem(4),
        out_specs=tuple(vmem(3)),
        name="unpack",
    )(rec, ksum, gradient, perm)
    return grad_signal[None], grad_gate[None], grad_filter


def solution(mesh):
    placed = (
        P("dp", "seq", None),
        P("dp", "seq", None),
        P("dp", "seq", None),
        P(None, "seq", "dp"),
    )
    return jax.shard_map(
        on_device,
        mesh=mesh,
        in_specs=placed,
        out_specs=(P("dp", "seq", None), P("dp", "seq", None), P(None, "seq", "dp")),
        check_vma=False,
    )
```

time: 227 us -> 62.1 us (0.27); the launches traced: 223 us -> 61.9 us
  matrix products: 80.4 us -> 0 us
  starting transfers between devices: 66.6 us -> 0 us
  Pallas kernels: 0 us -> 61.3 us
  waiting for transfers between devices: 48.4 us -> 0 us
  local copies, waits for them, and re-layouts: 21.8 us -> 0 us
  other arithmetic: 3.87 us -> 0 us
    dot_general x66 -> x0, matrix products: 80.4 us -> none  [the longest x44 56.6 us: right_product(): return jnp.einsum('ckq,qm->ckm', values, matrix, precision=highest)]
    all_to_all x10 -> x0, starting transfers between devices: 66.6 us -> none  [the longest x2 21.5 us: on_device(): lax.all_to_all(adjoint.astype(jnp.bfloat16).T, 'seq', split_axis=0, conca...]
    pallas_call x0 -> x5, Pallas kernels: none -> 61.3 us  [the longest x1 25.3 us: on_device(): pl.pallas_call(scatter_kernel, out_shape=(jax.ShapeDtypeStruct((pieces, 2...]
    all_to_all x10 -> x0, waiting for transfers between devices: 48.4 us -> none  [the longest x2 15.7 us: on_device(): lax.all_to_all(convolved.astype(jnp.bfloat16).T, 'seq', split_axis=0, con...]
    unnamed x82 -> x0, local copies, waits for them, and re-layouts: 10.9 us -> none
    all_to_all x6 -> x0, local copies, waits for them, and re-layouts: 3.73 us -> none  [the longest x2 1.38 us: on_device(): lax.all_to_all(scaled[:, segment], 'seq', split_axis=1, concat_axis=0, ti...]
    transpose x2 -> x0, local copies, waits for them, and re-layouts: 2.6 us -> none  [the longest x1 1.45 us: in_order(): return jnp.moveaxis(pieces, 0, dim).reshape(dims)]
    another operation x2 -> x0, local copies, waits for them, and re-layouts: 2.33 us -> none  [the longest x1 1.25 us: forward_dft(): blocks = values.astype(jnp.float32).reshape(stacked, kept_rows, columns)]
  transfers between devices with their start and end apart: 10 -> 0, of which waited for: 8 -> 0; matrix products, arithmetic and copies ran while one was open for 29% -> 0% of each run, Pallas kernels for 0% -> 0%
where the time goes in v1:
time: 62.1 us; the launch traced here: 61.9 us
  Pallas kernels  61.3 us (99%)
  between operations  0.65 us (1%)
    pallas_call x1, Pallas kernels, on_device(): pl.pallas_call(scatter_kernel, out_shape=(jax.ShapeDtypeStruct((pieces, 2...  25.3 us
    pallas_call x1, Pallas kernels, on_device(): pl.pallas_call(gather_kernel, out_shape=(jax.ShapeDtypeStruct((pieces, 2...  19.4 us
    pallas_call x1, Pallas kernels, spectral(): pl.pallas_call(spectral_kernel, out_shape=(jax.ShapeDtypeStruct(recv.shap...  11.3 us
    pallas_call x1, Pallas kernels, on_device(): pl.pallas_call(pack_kernel, out_shape=(jax.ShapeDtypeStruct((pieces, 2 *...  2.68 us
    pallas_call x1, Pallas kernels, on_device(): pl.pallas_call(functools.partial(unpack_kernel, factor), out_shape=(jax.S...  2.62 us

profile of v1, /device:TPU:1, one launch (start us, length us, event | category | flops | bytes accessed | tf_op | source)
XLA Modules:
  0.0 61.9 jit_solution(11379396363731663503)
XLA Ops:
  0.6 2.7 %pack.1 = (bf16[64,16,256]{2,1,0:T(8,128)(2,1)}, f32[32,8,256]{2,1,0:T(8,128)}) custom-call(bf16[256,512]{1,0:T(8,128)(2,1)} %bitcast.7, bf16[256,512]{1,0:T(8,128)(2,1)} %bitcast.11, bf16[256,512]{1,0:T(8,128)(2,1)} %bitcast.12, f32[2,4,8192]{2,1,0:T(4,128)} %filters_ref.1, bf16[512,512]{1,0:T(8,128)(2,1)} %constant.17.clone.perm_ref), custom_call_target="tpu_custom_call" | custom-call | tf_op jit(solution)/shard_map/pack/pallas_call | solution.py:326
  3.3 25.3 %scatter.1 = (bf16[64,16,256]{2,1,0:T(8,128)(2,1)}, f32[64,8,256]{2,1,0:T(8,128)}) custom-call(bf16[64,16,256]{2,1,0:T(8,128)(2,1)} %get-tuple-element.14.pack_ref, f32[32,8,256]{2,1,0:T(8,128)} %get-tuple-element.15.pf_ref), custom_call_target="tpu_custom_call" | custom-call | tf_op jit(solution)/shard_map/scatter/pallas_call | solution.py:337
  28.6 11.3 %spectral.1 = (bf16[64,16,256]{2,1,0:T(8,128)(2,1)}, f32[512,256]{1,0:T(8,128)}) custom-call(bf16[64,16,256]{2,1,0:T(8,128)(2,1)} %get-tuple-element.16.recv_ref, f32[512,256]{1,0:T(8,128)} %bitcast.10, bf16[128,192]{1,0:T(8,128)(2,1)} %constant.12.clone.fwd_ref, bf16[64,384]{1,0:T(8,128)(2,1)} %constant.13.clone.back_ref, ...), custom_call_target="tpu_custom_call" | custom-call | tf_op jit(solution)/shard_map/spectral/pallas_call | solution.py:296
  39.9 19.4 %gather.1 = (bf16[64,16,256]{2,1,0:T(8,128)(2,1)}, f32[32,8,256]{2,1,0:T(8,128)}) custom-call(bf16[64,16,256]{2,1,0:T(8,128)(2,1)} %get-tuple-element.18.back_ref, f32[64,8,256]{2,1,0:T(8,128)} %bitcast.9), custom_call_target="tpu_custom_call" | custom-call | tf_op jit(solution)/shard_map/gather/pallas_call | solution.py:350
  59.3 2.6 %unpack.1 = (bf16[256,512]{1,0:T(8,128)(2,1)}, bf16[256,512]{1,0:T(8,128)(2,1)}, f32[2,4,8192]{2,1,0:T(4,128)}) custom-call(bf16[64,16,256]{2,1,0:T(8,128)(2,1)} %get-tuple-element.20.rec_ref, f32[32,8,256]{2,1,0:T(8,128)} %get-tuple-element.21.ksum_ref, bf16[256,512]{1,0:T(8,128)(2,1)} %bitcast.8, bf16[512,512]{1,0:T(8,128)(2,1)} %constant.17.clone.perm_ref), custom_call_target="tpu_custom_call" | custom-call | tf_op jit(solution)/shard_map/unpack/pallas_call | solution.py:363

commit v2 on v1

v2 whole, which is shorter than its diff:
```python
import functools
import math

import jax
import jax.numpy as jnp
import numpy as np
from jax import lax
from jax.experimental import pallas as pl
from jax.experimental.pallas import tpu as pltpu
from jax.sharding import PartitionSpec as P

MESH = pl.DeviceIdType.MESH
bf16 = jnp.bfloat16
f32 = jnp.float32

U = 256
HALF = U // 2


def split_table(table):
    high = jnp.asarray(table, f32).astype(bf16)
    low = (jnp.asarray(table, f32) - high.astype(f32)).astype(bf16)
    return high, low


def np_bf16(table):
    import ml_dtypes

    return np.asarray(table, np.float32).astype(ml_dtypes.bfloat16)


def np_split(table):
    high = np_bf16(table)
    low = np_bf16(np.asarray(table, np.float64) - high.astype(np.float64))
    return high, low


@functools.lru_cache(None)
def make_tables(rows):
    points = 2 * rows * U
    k1 = np.arange(rows)[:, None]
    i = np.arange(rows)[None, :]
    angle = 2 * np.pi * (i * (2 * k1 + 1) % (4 * rows)) / (4 * rows)
    outer = np.concatenate([np.cos(angle), -np.sin(angle)], 0)
    high, low = np_split(outer)
    forward = np.concatenate([high, low, high], 1)
    back_high, back_low = np_split(outer.T * (2.0 / points))
    back = np.concatenate([back_high, back_low, back_high], 1)
    u = np.arange(U)[None, :]
    turn = 2 * np.pi * (u * (2 * k1 + 1)) / (2 * points)
    twiddle = np.stack([np.cos(turn), -np.sin(turn)]).astype(np.float32)
    u0 = np.arange(HALF)[:, None]
    m = np.arange(HALF)[None, :]
    inner = []
    for p in range(2):
        a = 2 * np.pi * (u0 * (2 * m + p) % U) / U
        c, s = np.cos(a), np.sin(a)
        inner.append(np.block([[c, -s], [s, c]]))
    inner = np.stack(inner)
    inner_tables = np.stack(np_split(inner), 1)
    inverse_tables = np.stack(np_split(np.swapaxes(inner, 1, 2)), 1)
    return forward, back, twiddle, inner_tables, inverse_tables


@functools.lru_cache(None)
def make_permutation(pieces, per_device):
    width = pieces * per_device
    row = np.arange(2 * width)
    j, rest = np.divmod(row, 2 * per_device)
    tensor, c = np.divmod(rest, per_device)
    table = np.zeros((2 * width, 2 * width), np.float32)
    table[row, tensor * width + j * per_device + c] = 1
    return np_bf16(table)


def dot(a, b, dims=((1,), (0,))):
    return lax.dot_general(a, b, (dims, ((), ())), preferred_element_type=f32)


def split(x):
    high = x.astype(bf16)
    return high, (x - high.astype(f32)).astype(bf16)


def peer_copy(src_ref, dst_ref, send_sem, recv_sem, peer):
    return pltpu.make_async_remote_copy(
        src_ref=src_ref,
        dst_ref=dst_ref,
        send_sem=send_sem,
        recv_sem=recv_sem,
        device_id=peer,
        device_id_type=MESH,
    )


def start_exchange(src_ref, dst_ref, send_sem, recv_sem):
    me = lax.axis_index("seq")
    pieces = src_ref.shape[0]

    def step(d, carry):
        peer = lax.rem(me + d, pieces)
        peer_copy(
            src_ref.at[peer], dst_ref.at[me], send_sem, recv_sem, {"seq": peer}
        ).start()
        return carry

    lax.fori_loop(1, pieces, step, 0)
    dst_ref[me] = src_ref[me]


def all_of(src_ref, dst_ref, send_sem, recv_sem):
    others = pl.ds(0, src_ref.shape[0] - 1)
    return peer_copy(
        src_ref.at[others],
        dst_ref.at[others],
        send_sem,
        recv_sem,
        {"seq": lax.axis_index("seq")},
    )


def greet_all(pieces):
    me = lax.axis_index("seq")
    barrier = pltpu.get_barrier_semaphore()

    def greet(d, carry):
        pl.semaphore_signal(
            barrier, inc=1, device_id={"seq": lax.rem(me + d, pieces)}, device_id_type=MESH
        )
        return carry

    lax.fori_loop(1, pieces, greet, 0)
    pl.semaphore_signal(
        barrier, inc=1, device_id={"dp": 1 - lax.axis_index("dp")}, device_id_type=MESH
    )
    return barrier


def take(ref, c, rows, stride):
    return jnp.concatenate([ref[h, pl.ds(c, rows, stride=stride), :] for h in range(2)], 1)


def put(ref, c, rows, stride, value):
    for h in range(2):
        ref[h, pl.ds(c, rows, stride=stride), :] = value[:, h * HALF : (h + 1) * HALF]


def turn(p, tw_ref):
    rows = p.shape[0] // 2
    pr, pi = p[:rows], p[rows:]
    tr, ti = tw_ref[0], tw_ref[1]
    qr = pr * tr - pi * ti
    qi = pr * ti + pi * tr
    a = jnp.concatenate([qr[:, :HALF], qi[:, :HALF]], 1)
    b = jnp.concatenate([qr[:, HALF:], qi[:, HALF:]], 1)
    return a + b, a - b


def unturn(plus, minus, tw_ref):
    tr, ti = tw_ref[0], tw_ref[1]
    zr = jnp.concatenate([plus[:, :HALF], minus[:, :HALF]], 1)
    zi = jnp.concatenate([plus[:, HALF:], minus[:, HALF:]], 1)
    return jnp.concatenate([zr * tr + zi * ti, zi * tr - zr * ti], 0)


def three(x, table_ref, p):
    high, low = split(x)
    return dot(high, table_ref[p, 0]) + dot(low, table_ref[p, 0]) + dot(high, table_ref[p, 1])


def main_kernel(
    grad_ref,
    gate_ref,
    signal_ref,
    filters_ref,
    perm_ref,
    fwd_ref,
    inner_back_ref,
    tw_ref,
    in_ref,
    inv_ref,
    rec_ref,
    ksum_ref,
    pack,
    recv,
    back,
    pf,
    filt,
    fs,
    fspec,
    xs,
    ys,
    ks,
    ker,
    kbuf,
    send_in,
    recv_in,
    send_out,
    recv_out,
    fsend,
    frecv,
    ksend,
    krecv,
):
    segments, pieces, group, tokens = pack.shape
    per_device = group // 2
    rows = pieces * tokens // U
    part = pf.shape[1]
    dp = lax.axis_index("dp")
    partner = {"dp": 1 - dp}
    barrier = greet_all(pieces)

    for s in range(segments):
        for i in range(part // per_device):
            pf[s, i * per_device : (i + 1) * per_device, :] = filters_ref[
                s, :, i * U : (i + 1) * U
            ]
    width = pieces * per_device
    for s in range(segments):
        here = slice(s * width, (s + 1) * width)
        scaled = (grad_ref[:, here].astype(f32) * gate_ref[:, here].astype(f32)).astype(bf16)
        joined = jnp.concatenate([scaled, signal_ref[:, here]], 1)
        moved = dot(perm_ref[...], joined, ((1,), (1,)))
        pack[s] = moved.reshape(pieces, group, tokens).astype(bf16)

    pl.semaphore_wait(barrier, pieces)
    mine = filt.at[:, pl.ds(dp * part, part)]
    filter_copy = peer_copy(pf, mine, fsend, frecv, partner)
    filter_copy.start()
    for s in range(segments):
        start_exchange(pack.at[s], recv.at[s], send_in.at[s], recv_in.at[s])
    mine[...] = pf[...]
    filter_copy.wait()

    for h in range(2):
        lanes = slice(h * HALF, (h + 1) * HALF)
        for s in range(segments):
            fs[s, h] = filt[s, :, lanes]

    for s in range(segments):

        def filter_step(n, carry, s=s):
            stages = []
            for c in (2 * n, 2 * n + 1):
                high, low = split(take(fs.at[s], c, rows, per_device))
                stages.append(
                    turn(dot(fwd_ref[...], jnp.concatenate([high, high, low], 0)), tw_ref)
                )
            at = pl.multiple_of(n * 2 * rows, 2 * rows)
            for p in range(2):
                fspec[s, p, pl.ds(at, 2 * rows)] = three(
                    jnp.concatenate([t[p] for t in stages], 0), in_ref, p
                )
            return carry

        lax.fori_loop(0, per_device // 2, filter_step, 0)

    short = fwd_ref[:, : 2 * rows]
    for s in range(segments):
        incoming = all_of(pack.at[s], recv.at[s], send_in.at[s], recv_in.at[s])
        incoming.wait_recv()
        for h in range(2):
            lanes = slice(h * HALF, (h + 1) * HALF)
            xs[h] = recv[s, :, :, lanes].astype(f32).reshape(rows * group, HALF)

        def step(c, carry, s=s):
            turned = []
            for r in (c, c + per_device):
                x = take(xs, r, rows, group).astype(bf16)
                turned.append(turn(dot(short, jnp.concatenate([x, x], 0)), tw_ref))
            at = pl.multiple_of(c * rows, rows)
            parts = []
            for p in range(2):
                spec = three(jnp.concatenate([t[p] for t in turned], 0), in_ref, p)
                fr = fspec[s, p, pl.ds(at, rows), :HALF]
                fi = fspec[s, p, pl.ds(at, rows), HALF:]
                gr, gi = spec[:rows, :HALF], spec[:rows, HALF:]
                sr, si = spec[rows:, :HALF], spec[rows:, HALF:]
                adj = jnp.concatenate([fr * gr + fi * gi, fr * gi - fi * gr], 1)
                conv = jnp.concatenate([fr * sr - fi * si, fr * si + fi * sr], 1)
                kernels = jnp.concatenate([gr * sr + gi * si, gi * sr - gr * si], 1)
                parts.append(three(jnp.concatenate([adj, conv, kernels], 0), inv_ref, p))
            plus, minus = parts[0] + parts[1], parts[0] - parts[1]
            results = []
            for n in range(3):
                here = slice(n * rows, (n + 1) * rows)
                high, low = split(unturn(plus[here], minus[here], tw_ref))
                results.append(
                    dot(inner_back_ref[...], jnp.concatenate([high, high, low], 0))
                )
            put(ys, c, rows, group, results[0])
            put(ys, c + per_device, rows, group, results[1])
            put(ks, c, rows, per_device, results[2])
            return carry

        lax.fori_loop(0, per_device, step, 0, unroll=UNROLL)
        for h in range(2):
            lanes = slice(h * HALF, (h + 1) * HALF)
            back[s, :, :, lanes] = ys[h].reshape(pieces, group, HALF).astype(bf16)
            ker[s, :, lanes] = ks[h]
        start_exchange(back.at[s], rec_ref.at[s], send_out.at[s], recv_out.at[s])
        peer_copy(
            ker.at[s, pl.ds((1 - dp) * part, part)], kbuf.at[s], ksend.at[s], krecv.at[s], partner
        ).start()

    for s in range(segments):
        peer_copy(
            ker.at[s, pl.ds((1 - dp) * part, part)], kbuf.at[s], ksend.at[s], krecv.at[s], partner
        ).wait()
        ksum_ref[s] = ker[s, pl.ds(dp * part, part)] + kbuf[s]
    for s in range(segments):
        all_of(pack.at[s], recv.at[s], send_in.at[s], recv_in.at[s]).wait_send()
        outgoing = all_of(back.at[s], rec_ref.at[s], send_out.at[s], recv_out.at[s])
        outgoing.wait_send()
        outgoing.wait_recv()


UNROLL = 2


def unpack_kernel(factor, rec_ref, ksum_ref, grad_ref, perm_ref, gs_ref, gg_ref, gf_ref):
    segments, pieces, group, tokens = rec_ref.shape
    per_device = group // 2
    width = pieces * per_device
    for s in range(segments):
        here = slice(s * width, (s + 1) * width)
        rec = rec_ref[s].astype(f32).reshape(pieces * group, tokens).astype(bf16)
        both = dot(rec, perm_ref[...], ((0,), (0,)))
        gs_ref[:, here] = both[:, :width].astype(bf16)
        gg_ref[:, here] = (grad_ref[:, here].astype(f32) * both[:, width:]).astype(bf16)
        for i in range(ksum_ref.shape[1] // per_device):
            gf_ref[s, :, i * U : (i + 1) * U] = (
                ksum_ref[s, i * per_device : (i + 1) * per_device, :] * factor
            )


def vmem(count):
    return [pl.BlockSpec(memory_space=pltpu.VMEM)] * count


def on_device(grad_out, gate, signal, filters):
    tokens, channels = grad_out.shape[1:]
    pieces = lax.axis_size("seq")
    halves = lax.axis_size("dp")
    segments, per_device, length = filters.shape
    group = 2 * per_device
    rows = length * halves // U
    part = length // U * per_device
    tables = [jnp.asarray(t) for t in make_tables(rows)]
    perm = jnp.asarray(make_permutation(pieces, per_device))
    gradient = grad_out[0]
    dma = pltpu.SemaphoreType.DMA
    blocks = (segments, pieces, group, tokens)
    rec, ksum = pl.pallas_call(
        main_kernel,
        out_shape=(
            jax.ShapeDtypeStruct(blocks, bf16),
            jax.ShapeDtypeStruct((segments, part, U), f32),
        ),
        in_specs=vmem(10),
        out_specs=tuple(vmem(2)),
        scratch_shapes=[
            pltpu.VMEM(blocks, bf16),
            pltpu.VMEM(blocks, bf16),
            pltpu.VMEM(blocks, bf16),
            pltpu.VMEM((segments, part, U), f32),
            pltpu.VMEM((segments, part * halves, U), f32),
            pltpu.VMEM((segments, 2, rows * per_device, HALF), f32),
            pltpu.VMEM((segments, 2, rows * per_device, U), f32),
            pltpu.VMEM((2, rows * group, HALF), f32),
            pltpu.VMEM((2, rows * group, HALF), f32),
            pltpu.VMEM((2, rows * per_device, HALF), f32),
            pltpu.VMEM((segments, part * halves, U), f32),
            pltpu.VMEM((segments, part, U), f32),
            dma((segments,)),
            dma((segments,)),
            dma((segments,)),
            dma((segments,)),
            dma,
            dma,
            dma((segments,)),
            dma((segments,)),
        ],
        compiler_params=pltpu.CompilerParams(collective_id=0, has_side_effects=True),
        name="main",
    )(gradient, gate[0], signal[0], filters, perm, *tables)
    factor = (halves * rows * U) ** (-0.5)
    grad_signal, grad_gate, grad_filter = pl.pallas_call(
        functools.partial(unpack_kernel, factor),
        out_shape=(
            jax.ShapeDtypeStruct((tokens, channels), bf16),
            jax.ShapeDtypeStruct((tokens, channels), bf16),
            jax.ShapeDtypeStruct(filters.shape, f32),
        ),
        in_specs=vmem(4),
        out_specs=tuple(vmem(3)),
        name="unpack",
    )(rec, ksum, gradient, perm)
    return grad_signal[None], grad_gate[None], grad_filter


def solution(mesh):
    placed = (
        P("dp", "seq", None),
        P("dp", "seq", None),
        P("dp", "seq", None),
        P(None, "seq", "dp"),
    )
    return jax.shard_map(
        on_device,
        mesh=mesh,
        in_specs=placed,
        out_specs=(P("dp", "seq", None), P("dp", "seq", None), P(None, "seq", "dp")),
        check_vma=False,
    )
```

time: 62.1 us -> 48.3 us (0.78)
  Pallas kernels: 61.3 us -> 47.5 us
    pallas_call x4 -> x1, Pallas kernels: 58.6 us -> 44.8 us  [on_device(): pl.pallas_call(main_kernel, out_shape=(jax.ShapeDtypeStruct(blocks, bf16)...]
where the time goes in v2:
time: 48.3 us; the launch traced here: 48.1 us
  Pallas kernels  47.5 us (98%)
  between operations  0.64 us (1%)
    pallas_call x1, Pallas kernels, on_device(): pl.pallas_call(main_kernel, out_shape=(jax.ShapeDtypeStruct(blocks, bf16)...  44.8 us
    pallas_call x1, Pallas kernels, on_device(): pl.pallas_call(functools.partial(unpack_kernel, factor), out_shape=(jax.S...  2.71 us

profile of v2, /device:TPU:1, one launch (start us, length us, event | category | flops | bytes accessed | tf_op | source)
XLA Modules:
  0.0 48.1 jit_solution(3340783663054000909)
XLA Ops:
  0.6 44.8 %main.1 = (bf16[2,64,8,256]{3,2,1,0:T(8,128)(2,1)}, f32[2,128,256]{2,1,0:T(8,128)}) custom-call(bf16[256,512]{1,0:T(8,128)(2,1)} %bitcast.5, bf16[256,512]{1,0:T(8,128)(2,1)} %bitcast.7, bf16[256,512]{1,0:T(8,128)(2,1)} %bitcast.8, f32[2,4,8192]{2,1,0:T(4,128)} %filters_ref.1, bf16[512,512]{1,0:T(8,128)(2,1)} %constant.17.clone.perm_ref, ...), custom_call_target="tpu_custom_call" | custom-call | tf_op jit(solution)/shard_map/main/pallas_call | solution.py:354
  45.4 2.7 %unpack.1 = (bf16[256,512]{1,0:T(8,128)(2,1)}, bf16[256,512]{1,0:T(8,128)(2,1)}, f32[2,4,8192]{2,1,0:T(4,128)}) custom-call(bf16[2,64,8,256]{3,2,1,0:T(8,128)(2,1)} %get-tuple-element.8.rec_ref, f32[2,128,256]{2,1,0:T(8,128)} %get-tuple-element.9.ksum_ref, bf16[256,512]{1,0:T(8,128)(2,1)} %bitcast.6, bf16[512,512]{1,0:T(8,128)(2,1)} %constant.17.clone.perm_ref), custom_call_target="tpu_custom_call" | custom-call | tf_op jit(solution)/shard_map/unpack/pallas_call | solution.py:388

commit v3 on v2

--- a/solution.py
+++ b/solution.py
@@ -93,12 +93,23 @@
     )
 
 
+def nth_peer(me, n, pieces):
+    def far(v):
+        return v + (v // 2) * (5 - 2 * v)
+
+    core = lax.rem(lax.rem(me, 2) + lax.rem(n, 2), 2)
+    x = lax.rem(lax.rem(me // 2, 4) + far(lax.rem(n // 2, 4)), 4)
+    y = lax.rem(lax.rem(me // 8, 4) + far(lax.rem(n // 8, 4)), 4)
+    z = lax.rem(me // 32 + n // 32, 2)
+    return ((z * 4 + y) * 4 + x) * 2 + core
+
+
 def start_exchange(src_ref, dst_ref, send_sem, recv_sem):
     me = lax.axis_index("seq")
     pieces = src_ref.shape[0]
 
-    def step(d, carry):
-        peer = lax.rem(me + d, pieces)
+    def step(n, carry):
+        peer = nth_peer(me, pieces - n, pieces)
         peer_copy(
             src_ref.at[peer], dst_ref.at[me], send_sem, recv_sem, {"seq": peer}
         ).start()
@@ -168,53 +179,40 @@
     return dot(high, table_ref[p, 0]) + dot(low, table_ref[p, 0]) + dot(high, table_ref[p, 1])
 
 
-def main_kernel(
-    grad_ref,
-    gate_ref,
-    signal_ref,
-    filters_ref,
-    perm_ref,
-    fwd_ref,
-    inner_back_ref,
-    tw_ref,
-    in_ref,
-    inv_ref,
-    rec_ref,
-    ksum_ref,
-    pack,
-    recv,
-    back,
-    pf,
-    filt,
-    fs,
-    fspec,
-    xs,
-    ys,
-    ks,
-    ker,
-    kbuf,
-    send_in,
-    recv_in,
-    send_out,
-    recv_out,
-    fsend,
-    frecv,
-    ksend,
-    krecv,
-):
+def main_kernel(*refs):
+    operands, refs = refs[:10], refs[10:]
+    rec_ref, ksum_ref = refs[:2]
+    held, refs = refs[2:12], refs[12:]
+    grad_ref, gate_ref, signal_ref, filters_ref, perm_ref = held[:5]
+    fwd_ref, inner_back_ref, tw_ref, in_ref, inv_ref = held[5:]
+    pack, recv, back, pf, pfin, fs, fspec, xs, ys, ks, kout, kbuf = refs[:12]
+    send_in, recv_in, send_out, recv_out, fsend, frecv, ksend, krecv, load_sem = refs[12:]
     segments, pieces, group, tokens = pack.shape
     per_device = group // 2
     rows = pieces * tokens // U
     part = pf.shape[1]
     dp = lax.axis_index("dp")
     partner = {"dp": 1 - dp}
+    loads = [
+        pltpu.make_async_copy(operands[n], held[n], load_sem.at[n]) for n in range(len(held))
+    ]
+    for n in (3, 0, 1, 2, 4, 5, 6, 7, 8, 9):
+        loads[n].start()
     barrier = greet_all(pieces)
 
+    loads[3].wait()
+    own = dp * part
+    other = (1 - dp) * part
     for s in range(segments):
         for i in range(part // per_device):
-            pf[s, i * per_device : (i + 1) * per_device, :] = filters_ref[
-                s, :, i * U : (i + 1) * U
-            ]
+            for h in range(2):
+                fs[s, h, pl.ds(own + i * per_device, per_device), :] = filters_ref[
+                    s, :, i * U + h * HALF : i * U + (h + 1) * HALF
+                ]
+        for h in range(2):
+            pf[s, :, h * HALF : (h + 1) * HALF] = fs[s, h, pl.ds(own, part)].astype(bf16)
+    for n in (0, 1, 2, 4):
+        loads[n].wait()
     width = pieces * per_device
     for s in range(segments):
         here = slice(s * width, (s + 1) * width)
@@ -224,18 +222,17 @@
         pack[s] = moved.reshape(pieces, group, tokens).astype(bf16)
 
     pl.semaphore_wait(barrier, pieces)
-    mine = filt.at[:, pl.ds(dp * part, part)]
-    filter_copy = peer_copy(pf, mine, fsend, frecv, partner)
+    filter_copy = peer_copy(pf, pfin, fsend, frecv, partner)
     filter_copy.start()
     for s in range(segments):
         start_exchange(pack.at[s], recv.at[s], send_in.at[s], recv_in.at[s])
-    mine[...] = pf[...]
+    for n in range(5, 10):
+        loads[n].wait()
     filter_copy.wait()
-
     for h in range(2):
         lanes = slice(h * HALF, (h + 1) * HALF)
         for s in range(segments):
-            fs[s, h] = filt[s, :, lanes]
+            fs[s, h, pl.ds(other, part)] = pfin[s, :, lanes].astype(f32)
 
     for s in range(segments):
 
@@ -290,24 +287,22 @@
                 )
             put(ys, c, rows, group, results[0])
             put(ys, c + per_device, rows, group, results[1])
-            put(ks, c, rows, per_device, results[2])
+            put(ks.at[s], c, rows, per_device, results[2])
             return carry
 
         lax.fori_loop(0, per_device, step, 0, unroll=UNROLL)
         for h in range(2):
             lanes = slice(h * HALF, (h + 1) * HALF)
             back[s, :, :, lanes] = ys[h].reshape(pieces, group, HALF).astype(bf16)
-            ker[s, :, lanes] = ks[h]
+            kout[s, :, lanes] = ks[s, h, pl.ds(other, part)].astype(bf16)
         start_exchange(back.at[s], rec_ref.at[s], send_out.at[s], recv_out.at[s])
-        peer_copy(
-            ker.at[s, pl.ds((1 - dp) * part, part)], kbuf.at[s], ksend.at[s], krecv.at[s], partner
-        ).start()
-
-    for s in range(segments):
-        peer_copy(
-            ker.at[s, pl.ds((1 - dp) * part, part)], kbuf.at[s], ksend.at[s], krecv.at[s], partner
-        ).wait()
-        ksum_ref[s] = ker[s, pl.ds(dp * part, part)] + kbuf[s]
+        peer_copy(kout.at[s], kbuf.at[s], ksend.at[s], krecv.at[s], partner).start()
+
+    for s in range(segments):
+        peer_copy(kout.at[s], kbuf.at[s], ksend.at[s], krecv.at[s], partner).wait()
+        for h in range(2):
+            lanes = slice(h * HALF, (h + 1) * HALF)
+            ksum_ref[s, :, lanes] = ks[s, h, pl.ds(own, part)] + kbuf[s, :, lanes].astype(f32)
     for s in range(segments):
         all_of(pack.at[s], recv.at[s], send_in.at[s], recv_in.at[s]).wait_send()
         outgoing = all_of(back.at[s], rec_ref.at[s], send_out.at[s], recv_out.at[s])
@@ -351,27 +346,29 @@
     gradient = grad_out[0]
     dma = pltpu.SemaphoreType.DMA
     blocks = (segments, pieces, group, tokens)
+    operands = (gradient, gate[0], signal[0], filters, perm, *tables)
     rec, ksum = pl.pallas_call(
         main_kernel,
         out_shape=(
             jax.ShapeDtypeStruct(blocks, bf16),
             jax.ShapeDtypeStruct((segments, part, U), f32),
         ),
-        in_specs=vmem(10),
+        in_specs=[pl.BlockSpec(memory_space=pltpu.HBM)] * 10,
         out_specs=tuple(vmem(2)),
-        scratch_shapes=[
+        scratch_shapes=[pltpu.VMEM(x.shape, x.dtype) for x in operands]
+        + [
             pltpu.VMEM(blocks, bf16),
             pltpu.VMEM(blocks, bf16),
             pltpu.VMEM(blocks, bf16),
-            pltpu.VMEM((segments, part, U), f32),
-            pltpu.VMEM((segments, part * halves, U), f32),
+            pltpu.VMEM((segments, part, U), bf16),
+            pltpu.VMEM((segments, part, U), bf16),
             pltpu.VMEM((segments, 2, rows * per_device, HALF), f32),
             pltpu.VMEM((segments, 2, rows * per_device, U), f32),
             pltpu.VMEM((2, rows * group, HALF), f32),
             pltpu.VMEM((2, rows * group, HALF), f32),
-            pltpu.VMEM((2, rows * per_device, HALF), f32),
-            pltpu.VMEM((segments, part * halves, U), f32),
-            pltpu.VMEM((segments, part, U), f32),
+            pltpu.VMEM((segments, 2, rows * per_device, HALF), f32),
+            pltpu.VMEM((segments, part, U), bf16),
+            pltpu.VMEM((segments, part, U), bf16),
             dma((segments,)),
             dma((segments,)),
             dma((segments,)),
@@ -380,10 +377,13 @@
             dma,
             dma((segments,)),
             dma((segments,)),
+            dma((len(operands),)),
         ],
-        compiler_params=pltpu.CompilerParams(collective_id=0, has_side_effects=True),
+        compiler_params=pltpu.CompilerParams(
+            collective_id=0, has_side_effects=True, vmem_limit_bytes=60 << 20
+        ),
         name="main",
-    )(gradient, gate[0], signal[0], filters, perm, *tables)
+    )(*operands)
     factor = (halves * rows * U) ** (-0.5)
     grad_signal, grad_gate, grad_filter = pl.pallas_call(
         functools.partial(unpack_kernel, factor),

time: 48.3 us -> 44.2 us (0.915)
  Pallas kernels: 47.5 us -> 43.4 us
    pallas_call x1, Pallas kernels: 44.8 us -> 40.6 us  [on_device(): pl.pallas_call(main_kernel, out_shape=(jax.ShapeDtypeStruct(blocks, bf16)...]
where the time goes in v3:
time: 44.2 us; the launch traced here: 44 us
  Pallas kernels  43.4 us (98%)
  between operations  0.64 us (1%)
    pallas_call x1, Pallas kernels, on_device(): pl.pallas_call(main_kernel, out_shape=(jax.ShapeDtypeStruct(blocks, bf16)...  40.6 us
    pallas_call x1, Pallas kernels, on_device(): pl.pallas_call(functools.partial(unpack_kernel, factor), out_shape=(jax.S...  2.71 us

profile of v3, /device:TPU:1, one launch (start us, length us, event | category | flops | bytes accessed | tf_op | source)
XLA Modules:
  0.0 44.0 jit_solution(11461124633528387014)
XLA Ops:
  0.6 40.6 %main.1 = (bf16[2,64,8,256]{3,2,1,0:T(8,128)(2,1)}, f32[2,128,256]{2,1,0:T(8,128)}) custom-call(bf16[256,512]{1,0:T(8,128)(2,1)} %bitcast.5, bf16[256,512]{1,0:T(8,128)(2,1)} %bitcast.7, bf16[256,512]{1,0:T(8,128)(2,1)} %bitcast.8, f32[2,4,8192]{2,1,0:T(4,128)} %refs_3_.1, bf16[512,512]{1,0:T(8,128)(2,1)} %constant.17.clone.refs_4_.perm_ref, ...), custom_call_target="tpu_custom_call" | custom-call | tf_op jit(solution)/shard_map/main/pallas_call | solution.py:350
  41.3 2.7 %unpack.1 = (bf16[256,512]{1,0:T(8,128)(2,1)}, bf16[256,512]{1,0:T(8,128)(2,1)}, f32[2,4,8192]{2,1,0:T(4,128)}) custom-call(bf16[2,64,8,256]{3,2,1,0:T(8,128)(2,1)} %get-tuple-element.8.rec_ref, f32[2,128,256]{2,1,0:T(8,128)} %get-tuple-element.9.ksum_ref, bf16[256,512]{1,0:T(8,128)(2,1)} %bitcast.6, bf16[512,512]{1,0:T(8,128)(2,1)} %constant.17.clone.refs_4_.perm_ref), custom_call_target="tpu_custom_call" | custom-call | tf_op jit(solution)/shard_map/unpack/pallas_call | solution.py:388

commit v4 on v3

--- a/solution.py
+++ b/solution.py
@@ -93,29 +93,47 @@
     )
 
 
-def nth_peer(me, n, pieces):
-    def far(v):
-        return v + (v // 2) * (5 - 2 * v)
-
-    core = lax.rem(lax.rem(me, 2) + lax.rem(n, 2), 2)
-    x = lax.rem(lax.rem(me // 2, 4) + far(lax.rem(n // 2, 4)), 4)
-    y = lax.rem(lax.rem(me // 8, 4) + far(lax.rem(n // 8, 4)), 4)
-    z = lax.rem(me // 32 + n // 32, 2)
-    return ((z * 4 + y) * 4 + x) * 2 + core
+def for_each_peer(visit):
+    me = lax.axis_index("seq")
+    far = (2, 3, 1, 0)
+
+    def part(divisor, size):
+        return lax.rem(lax.div(me, jnp.int32(divisor)), jnp.int32(size))
+
+    core, x, y, z = part(1, 2), part(2, 4), part(8, 4), part(32, 2)
+    low = [
+        lax.rem(x + dx, jnp.int32(4)) * 2 + lax.rem(core + dc, jnp.int32(2))
+        for dx in far
+        for dc in (1, 0)
+    ]
+    z_other = (1 - z) * 32
+
+    def row(base, targets):
+        for target in targets:
+            visit(base + target)
+
+    def far_rows(n, carry):
+        row(z_other + lax.rem(y + 2 + n, jnp.int32(4)) * 8, low)
+        return carry
+
+    def near_rows(n, carry):
+        row(z * 32 + lax.rem(y + 1 + n, jnp.int32(4)) * 8, low)
+        return carry
+
+    lax.fori_loop(0, 4, far_rows, 0)
+    lax.fori_loop(0, 3, near_rows, 0)
+    row(z * 32 + y * 8, low[:-1])
 
 
 def start_exchange(src_ref, dst_ref, send_sem, recv_sem):
     me = lax.axis_index("seq")
-    pieces = src_ref.shape[0]
-
-    def step(n, carry):
-        peer = nth_peer(me, pieces - n, pieces)
+
+    def send(peer):
         peer_copy(
             src_ref.at[peer], dst_ref.at[me], send_sem, recv_sem, {"seq": peer}
         ).start()
-        return carry
-
-    lax.fori_loop(1, pieces, step, 0)
+
+    for_each_peer(send)
     dst_ref[me] = src_ref[me]
 
 
@@ -130,17 +148,13 @@
     )
 
 
-def greet_all(pieces):
-    me = lax.axis_index("seq")
+def greet_all():
     barrier = pltpu.get_barrier_semaphore()
 
-    def greet(d, carry):
-        pl.semaphore_signal(
-            barrier, inc=1, device_id={"seq": lax.rem(me + d, pieces)}, device_id_type=MESH
-        )
-        return carry
-
-    lax.fori_loop(1, pieces, greet, 0)
+    def greet(peer):
+        pl.semaphore_signal(barrier, inc=1, device_id={"seq": peer}, device_id_type=MESH)
+
+    for_each_peer(greet)
     pl.semaphore_signal(
         barrier, inc=1, device_id={"dp": 1 - lax.axis_index("dp")}, device_id_type=MESH
     )
@@ -198,7 +212,7 @@
     ]
     for n in (3, 0, 1, 2, 4, 5, 6, 7, 8, 9):
         loads[n].start()
-    barrier = greet_all(pieces)
+    barrier = greet_all()
 
     loads[3].wait()
     own = dp * part
@@ -260,37 +274,45 @@
             lanes = slice(h * HALF, (h + 1) * HALF)
             xs[h] = recv[s, :, :, lanes].astype(f32).reshape(rows * group, HALF)
 
-        def step(c, carry, s=s):
+        def step(n, carry, s=s):
+            channels = [n * BATCHED + k for k in range(BATCHED)]
             turned = []
-            for r in (c, c + per_device):
-                x = take(xs, r, rows, group).astype(bf16)
-                turned.append(turn(dot(short, jnp.concatenate([x, x], 0)), tw_ref))
-            at = pl.multiple_of(c * rows, rows)
+            for c in channels:
+                for r in (c, c + per_device):
+                    x = take(xs, r, rows, group).astype(bf16)
+                    turned.append(turn(dot(short, jnp.concatenate([x, x], 0)), tw_ref))
             parts = []
             for p in range(2):
                 spec = three(jnp.concatenate([t[p] for t in turned], 0), in_ref, p)
-                fr = fspec[s, p, pl.ds(at, rows), :HALF]
-                fi = fspec[s, p, pl.ds(at, rows), HALF:]
-                gr, gi = spec[:rows, :HALF], spec[:rows, HALF:]
-                sr, si = spec[rows:, :HALF], spec[rows:, HALF:]
-                adj = jnp.concatenate([fr * gr + fi * gi, fr * gi - fi * gr], 1)
-                conv = jnp.concatenate([fr * sr - fi * si, fr * si + fi * sr], 1)
-                kernels = jnp.concatenate([gr * sr + gi * si, gi * sr - gr * si], 1)
-                parts.append(three(jnp.concatenate([adj, conv, kernels], 0), inv_ref, p))
+                products = []
+                for k, c in enumerate(channels):
+                    at = pl.multiple_of(c * rows, rows)
+                    fr = fspec[s, p, pl.ds(at, rows), :HALF]
+                    fi = fspec[s, p, pl.ds(at, rows), HALF:]
+                    g = spec[2 * k * rows : (2 * k + 1) * rows]
+                    x = spec[(2 * k + 1) * rows : (2 * k + 2) * rows]
+                    gr, gi, sr, si = g[:, :HALF], g[:, HALF:], x[:, :HALF], x[:, HALF:]
+                    products += [
+                        jnp.concatenate([fr * gr + fi * gi, fr * gi - fi * gr], 1),
+                        jnp.concatenate([fr * sr - fi * si, fr * si + fi * sr], 1),
+                        jnp.concatenate([gr * sr + gi * si, gi * sr - gr * si], 1),
+                    ]
+                parts.append(three(jnp.concatenate(products, 0), inv_ref, p))
             plus, minus = parts[0] + parts[1], parts[0] - parts[1]
-            results = []
-            for n in range(3):
-                here = slice(n * rows, (n + 1) * rows)
-                high, low = split(unturn(plus[here], minus[here], tw_ref))
-                results.append(
-                    dot(inner_back_ref[...], jnp.concatenate([high, high, low], 0))
-                )
-            put(ys, c, rows, group, results[0])
-            put(ys, c + per_device, rows, group, results[1])
-            put(ks.at[s], c, rows, per_device, results[2])
+            for k, c in enumerate(channels):
+                results = []
+                for m in range(3):
+                    here = slice((3 * k + m) * rows, (3 * k + m + 1) * rows)
+                    high, low = split(unturn(plus[here], minus[here], tw_ref))
+                    results.append(
+                        dot(inner_back_ref[...], jnp.concatenate([high, high, low], 0))
+                    )
+                put(ys, c, rows, group, results[0])
+                put(ys, c + per_device, rows, group, results[1])
+                put(ks.at[s], c, rows, per_device, results[2])
             return carry
 
-        lax.fori_loop(0, per_device, step, 0, unroll=UNROLL)
+        lax.fori_loop(0, per_device // BATCHED, step, 0, unroll=UNROLL)
         for h in range(2):
             lanes = slice(h * HALF, (h + 1) * HALF)
             back[s, :, :, lanes] = ys[h].reshape(pieces, group, HALF).astype(bf16)
@@ -310,7 +332,8 @@
         outgoing.wait_recv()
 
 
-UNROLL = 2
+UNROLL = 1
+BATCHED = 4
 
 
 def unpack_kernel(factor, rec_ref, ksum_ref, grad_ref, perm_ref, gs_ref, gg_ref, gf_ref):

time: 44.2 us -> 39.5 us (0.89)
  Pallas kernels: 43.4 us -> 38.7 us
    pallas_call x1, Pallas kernels: 40.6 us -> 36 us  [on_device(): pl.pallas_call(main_kernel, out_shape=(jax.ShapeDtypeStruct(blocks, bf16)...]
where the time goes in v4:
time: 39.5 us; the launch traced here: 39.4 us
  Pallas kernels  38.7 us (98%)
  between operations  0.64 us (2%)
    pallas_call x1, Pallas kernels, on_device(): pl.pallas_call(main_kernel, out_shape=(jax.ShapeDtypeStruct(blocks, bf16)...  36 us
    pallas_call x1, Pallas kernels, on_device(): pl.pallas_call(functools.partial(unpack_kernel, factor), out_shape=(jax.S...  2.71 us

profile of v4, /device:TPU:1, one launch (start us, length us, event | category | flops | bytes accessed | tf_op | source)
XLA Modules:
  0.0 39.4 jit_solution(7623338801019163451)
XLA Ops:
  0.6 36.0 %main.1 = (bf16[2,64,8,256]{3,2,1,0:T(8,128)(2,1)}, f32[2,128,256]{2,1,0:T(8,128)}) custom-call(bf16[256,512]{1,0:T(8,128)(2,1)} %bitcast.5, bf16[256,512]{1,0:T(8,128)(2,1)} %bitcast.7, bf16[256,512]{1,0:T(8,128)(2,1)} %bitcast.8, f32[2,4,8192]{2,1,0:T(4,128)} %refs_3_.1, bf16[512,512]{1,0:T(8,128)(2,1)} %constant.17.clone.refs_4_.perm_ref, ...), custom_call_target="tpu_custom_call" | custom-call | tf_op jit(solution)/shard_map/main/pallas_call | solution.py:373
  36.7 2.7 %unpack.1 = (bf16[256,512]{1,0:T(8,128)(2,1)}, bf16[256,512]{1,0:T(8,128)(2,1)}, f32[2,4,8192]{2,1,0:T(4,128)}) custom-call(bf16[2,64,8,256]{3,2,1,0:T(8,128)(2,1)} %get-tuple-element.8.rec_ref, f32[2,128,256]{2,1,0:T(8,128)} %get-tuple-element.9.ksum_ref, bf16[256,512]{1,0:T(8,128)(2,1)} %bitcast.6, bf16[512,512]{1,0:T(8,128)(2,1)} %constant.17.clone.refs_4_.perm_ref), custom_call_target="tpu_custom_call" | custom-call | tf_op jit(solution)/shard_map/unpack/pallas_call | solution.py:411

commit v5 on v4

--- a/solution.py
+++ b/solution.py
@@ -193,14 +193,16 @@
     return dot(high, table_ref[p, 0]) + dot(low, table_ref[p, 0]) + dot(high, table_ref[p, 1])
 
 
-def main_kernel(*refs):
+def main_kernel(factor, *refs):
     operands, refs = refs[:10], refs[10:]
-    rec_ref, ksum_ref = refs[:2]
-    held, refs = refs[2:12], refs[12:]
+    outs, refs = refs[:3], refs[3:]
+    held, refs = refs[:10], refs[10:]
     grad_ref, gate_ref, signal_ref, filters_ref, perm_ref = held[:5]
     fwd_ref, inner_back_ref, tw_ref, in_ref, inv_ref = held[5:]
-    pack, recv, back, pf, pfin, fs, fspec, xs, ys, ks, kout, kbuf = refs[:12]
-    send_in, recv_in, send_out, recv_out, fsend, frecv, ksend, krecv, load_sem = refs[12:]
+    pack, recv, back, rec, pf, pfin, fs, fspec, xs, ys, ks, ksum, kout, kbuf = refs[:14]
+    made, refs = refs[14:17], refs[17:]
+    gs, gg, gf = made
+    send_in, recv_in, send_out, recv_out, fsend, frecv, ksend, krecv, load_sem, store_sem = refs
     segments, pieces, group, tokens = pack.shape
     per_device = group // 2
     rows = pieces * tokens // U
@@ -317,43 +319,63 @@
             lanes = slice(h * HALF, (h + 1) * HALF)
             back[s, :, :, lanes] = ys[h].reshape(pieces, group, HALF).astype(bf16)
             kout[s, :, lanes] = ks[s, h, pl.ds(other, part)].astype(bf16)
-        start_exchange(back.at[s], rec_ref.at[s], send_out.at[s], recv_out.at[s])
+        start_exchange(back.at[s], rec.at[s], send_out.at[s], recv_out.at[s])
         peer_copy(kout.at[s], kbuf.at[s], ksend.at[s], krecv.at[s], partner).start()
+
+    stores = []
+
+    def store(n, s, at):
+        copy = pltpu.make_async_copy(made[n].at[at], outs[n].at[at], store_sem.at[n, s])
+        copy.start()
+        stores.append(copy)
 
     for s in range(segments):
         peer_copy(kout.at[s], kbuf.at[s], ksend.at[s], krecv.at[s], partner).wait()
         for h in range(2):
             lanes = slice(h * HALF, (h + 1) * HALF)
-            ksum_ref[s, :, lanes] = ks[s, h, pl.ds(own, part)] + kbuf[s, :, lanes].astype(f32)
+            mine = ks[s, h, pl.ds(own, part)]
+            ksum[h] = (mine + kbuf[s, :, lanes].astype(f32)) * factor
+            for i in range(part // per_device):
+                gf[s, :, i * U + h * HALF : i * U + (h + 1) * HALF] = ksum[
+                    h, i * per_device : (i + 1) * per_device, :
+                ]
+        store(2, s, (s,))
+        all_of(back.at[s], rec.at[s], send_out.at[s], recv_out.at[s]).wait_recv()
+        here = slice(s * width, (s + 1) * width)
+        arrived = rec[s].astype(f32).reshape(pieces * group, tokens).astype(bf16)
+        both = dot(arrived, perm_ref[...], ((0,), (0,)))
+        gs[:, here] = both[:, :width].astype(bf16)
+        gg[:, here] = (grad_ref[:, here].astype(f32) * both[:, width:]).astype(bf16)
+        at = (slice(None), pl.ds(s * width, width))
+        store(0, s, at)
+        store(1, s, at)
     for s in range(segments):
         all_of(pack.at[s], recv.at[s], send_in.at[s], recv_in.at[s]).wait_send()
-        outgoing = all_of(back.at[s], rec_ref.at[s], send_out.at[s], recv_out.at[s])
-        outgoing.wait_send()
-        outgoing.wait_recv()
+        all_of(back.at[s], rec.at[s], send_out.at[s], recv_out.at[s]).wait_send()
+    for copy in stores:
+        copy.wait()
 
 
 UNROLL = 1
 BATCHED = 4
 
 
-def unpack_kernel(factor, rec_ref, ksum_ref, grad_ref, perm_ref, gs_ref, gg_ref, gf_ref):
-    segments, pieces, group, tokens = rec_ref.shape
-    per_device = group // 2
-    width = pieces * per_device
-    for s in range(segments):
-        here = slice(s * width, (s + 1) * width)
-        rec = rec_ref[s].astype(f32).reshape(pieces * group, tokens).astype(bf16)
-        both = dot(rec, perm_ref[...], ((0,), (0,)))
-        gs_ref[:, here] = both[:, :width].astype(bf16)
-        gg_ref[:, here] = (grad_ref[:, here].astype(f32) * both[:, width:]).astype(bf16)
-        for i in range(ksum_ref.shape[1] // per_device):
-            gf_ref[s, :, i * U : (i + 1) * U] = (
-                ksum_ref[s, i * per_device : (i + 1) * per_device, :] * factor
-            )
-
-
-def vmem(count):
-    return [pl.BlockSpec(memory_space=pltpu.VMEM)] * count
+def finish_kernel(*refs):
+    sources, outs, held = refs[:3], refs[3:6], refs[6:9]
+    sems = refs[9]
+    loads = [pltpu.make_async_copy(sources[n], held[n], sems.at[0, n]) for n in range(3)]
+    stores = [pltpu.make_async_copy(held[n], outs[n], sems.at[1, n]) for n in range(3)]
+    for copy in loads:
+        copy.start()
+    for n in range(3):
+        loads[n].wait()
+        stores[n].start()
+    for copy in stores:
+        copy.wait()
+
+
+def hbm(count):
+    return [pl.BlockSpec(memory_space=pltpu.HBM)] * count
 
 
 def on_device(grad_out, gate, signal, filters):
@@ -370,16 +392,20 @@
     dma = pltpu.SemaphoreType.DMA
     blocks = (segments, pieces, group, tokens)
     operands = (gradient, gate[0], signal[0], filters, perm, *tables)
-    rec, ksum = pl.pallas_call(
-        main_kernel,
-        out_shape=(
-            jax.ShapeDtypeStruct(blocks, bf16),
-            jax.ShapeDtypeStruct((segments, part, U), f32),
-        ),
-        in_specs=[pl.BlockSpec(memory_space=pltpu.HBM)] * 10,
-        out_specs=tuple(vmem(2)),
+    factor = (halves * rows * U) ** (-0.5)
+    results = (
+        jax.ShapeDtypeStruct((tokens, channels), bf16),
+        jax.ShapeDtypeStruct((tokens, channels), bf16),
+        jax.ShapeDtypeStruct(filters.shape, f32),
+    )
+    made = pl.pallas_call(
+        functools.partial(main_kernel, factor),
+        out_shape=results,
+        in_specs=hbm(10),
+        out_specs=tuple(hbm(3)),
         scratch_shapes=[pltpu.VMEM(x.shape, x.dtype) for x in operands]
         + [
+            pltpu.VMEM(blocks, bf16),
             pltpu.VMEM(blocks, bf16),
             pltpu.VMEM(blocks, bf16),
             pltpu.VMEM(blocks, bf16),
@@ -390,8 +416,10 @@
             pltpu.VMEM((2, rows * group, HALF), f32),
             pltpu.VMEM((2, rows * group, HALF), f32),
             pltpu.VMEM((segments, 2, rows * per_device, HALF), f32),
+            pltpu.VMEM((2, part, HALF), f32),
             pltpu.VMEM((segments, part, U), bf16),
             pltpu.VMEM((segments, part, U), bf16),
+            *[pltpu.VMEM(x.shape, x.dtype) for x in results],
             dma((segments,)),
             dma((segments,)),
             dma((segments,)),
@@ -401,24 +429,21 @@
             dma((segments,)),
             dma((segments,)),
             dma((len(operands),)),
+            dma((3, segments)),
         ],
         compiler_params=pltpu.CompilerParams(
             collective_id=0, has_side_effects=True, vmem_limit_bytes=60 << 20
         ),
         name="main",
     )(*operands)
-    factor = (halves * rows * U) ** (-0.5)
     grad_signal, grad_gate, grad_filter = pl.pallas_call(
-        functools.partial(unpack_kernel, factor),
-        out_shape=(
-            jax.ShapeDtypeStruct((tokens, channels), bf16),
-            jax.ShapeDtypeStruct((tokens, channels), bf16),
-            jax.ShapeDtypeStruct(filters.shape, f32),
-        ),
-        in_specs=vmem(4),
-        out_specs=tuple(vmem(3)),
-        name="unpack",
-    )(rec, ksum, gradient, perm)
+        finish_kernel,
+        out_shape=results,
+        in_specs=hbm(3),
+        out_specs=tuple(hbm(3)),
+        scratch_shapes=[pltpu.VMEM(x.shape, x.dtype) for x in results] + [dma((2, 3))],
+        name="finish",
+    )(*made)
     return grad_signal[None], grad_gate[None], grad_filter
 
 

time: 39.5 us -> 38.9 us (0.985)
  Pallas kernels: 38.7 us -> 38.1 us
    pallas_call x2, Pallas kernels: 38.7 us -> 38.1 us  [the longest x1 36.2 us: on_device(): pl.pallas_call(functools.partial(main_kernel, factor), out_shape=results,...]
where the time goes in v5:
time: 38.9 us; the launch traced here: 38.8 us
  Pallas kernels  38.1 us (98%)
  between operations  0.64 us (2%)
    pallas_call x1, Pallas kernels, on_device(): pl.pallas_call(functools.partial(main_kernel, factor), out_shape=results,...  36.2 us
    pallas_call x1, Pallas kernels, on_device(): pl.pallas_call(finish_kernel, out_shape=results, in_specs=hbm(3), out_spe...  1.88 us

profile of v5, /device:TPU:1, one launch (start us, length us, event | category | flops | bytes accessed | tf_op | source)
XLA Modules:
  0.0 38.8 jit_solution(13203239391510890343)
XLA Ops:
  0.6 36.2 %main.1 = (bf16[256,512]{1,0:T(8,128)(2,1)}, bf16[256,512]{1,0:T(8,128)(2,1)}, f32[2,4,8192]{2,1,0:T(4,128)}) custom-call(bf16[256,512]{1,0:T(8,128)(2,1)} %bitcast.5, bf16[256,512]{1,0:T(8,128)(2,1)} %bitcast.6, bf16[256,512]{1,0:T(8,128)(2,1)} %bitcast.7, f32[2,4,8192]{2,1,0:T(4,128)} %refs_3_.1, bf16[512,512]{1,0:T(8,128)(2,1)} %constant.17.clone.refs_4_, ...), custom_call_target="tpu_custom_call" | custom-call | tf_op jit(solution)/shard_map/main/pallas_call | solution.py:401
  36.9 1.9 %finish.1 = (bf16[256,512]{1,0:T(8,128)(2,1)}, bf16[256,512]{1,0:T(8,128)(2,1)}, f32[2,4,8192]{2,1,0:T(4,128)}) custom-call(bf16[256,512]{1,0:T(8,128)(2,1)} %get-tuple-element.9.refs_0_, bf16[256,512]{1,0:T(8,128)(2,1)} %get-tuple-element.10.refs_1_, f32[2,4,8192]{2,1,0:T(4,128)} %get-tuple-element.11.refs_2_), custom_call_target="tpu_custom_call" | custom-call | tf_op jit(solution)/shard_map/finish/pallas_call | solution.py:439

commit v6 on v5

--- a/solution.py
+++ b/solution.py
@@ -238,19 +238,19 @@
         pack[s] = moved.reshape(pieces, group, tokens).astype(bf16)
 
     pl.semaphore_wait(barrier, pieces)
-    filter_copy = peer_copy(pf, pfin, fsend, frecv, partner)
-    filter_copy.start()
-    for s in range(segments):
+    filter_copies = [
+        peer_copy(pf.at[s], pfin.at[s], fsend.at[s], frecv.at[s], partner) for s in range(segments)
+    ]
+    for s in range(segments):
+        filter_copies[s].start()
         start_exchange(pack.at[s], recv.at[s], send_in.at[s], recv_in.at[s])
     for n in range(5, 10):
         loads[n].wait()
-    filter_copy.wait()
-    for h in range(2):
-        lanes = slice(h * HALF, (h + 1) * HALF)
-        for s in range(segments):
+    for s in range(segments):
+        filter_copies[s].wait()
+        for h in range(2):
+            lanes = slice(h * HALF, (h + 1) * HALF)
             fs[s, h, pl.ds(other, part)] = pfin[s, :, lanes].astype(f32)
-
-    for s in range(segments):
 
         def filter_step(n, carry, s=s):
             stages = []
@@ -276,51 +276,59 @@
             lanes = slice(h * HALF, (h + 1) * HALF)
             xs[h] = recv[s, :, :, lanes].astype(f32).reshape(rows * group, HALF)
 
-        def step(n, carry, s=s):
-            channels = [n * BATCHED + k for k in range(BATCHED)]
-            turned = []
-            for c in channels:
-                for r in (c, c + per_device):
-                    x = take(xs, r, rows, group).astype(bf16)
-                    turned.append(turn(dot(short, jnp.concatenate([x, x], 0)), tw_ref))
-            parts = []
-            for p in range(2):
-                spec = three(jnp.concatenate([t[p] for t in turned], 0), in_ref, p)
-                products = []
-                for k, c in enumerate(channels):
-                    at = pl.multiple_of(c * rows, rows)
-                    fr = fspec[s, p, pl.ds(at, rows), :HALF]
-                    fi = fspec[s, p, pl.ds(at, rows), HALF:]
-                    g = spec[2 * k * rows : (2 * k + 1) * rows]
-                    x = spec[(2 * k + 1) * rows : (2 * k + 2) * rows]
-                    gr, gi, sr, si = g[:, :HALF], g[:, HALF:], x[:, :HALF], x[:, HALF:]
-                    products += [
-                        jnp.concatenate([fr * gr + fi * gi, fr * gi - fi * gr], 1),
-                        jnp.concatenate([fr * sr - fi * si, fr * si + fi * sr], 1),
-                        jnp.concatenate([gr * sr + gi * si, gi * sr - gr * si], 1),
-                    ]
-                parts.append(three(jnp.concatenate(products, 0), inv_ref, p))
-            plus, minus = parts[0] + parts[1], parts[0] - parts[1]
-            for k, c in enumerate(channels):
-                results = []
-                for m in range(3):
-                    here = slice((3 * k + m) * rows, (3 * k + m + 1) * rows)
-                    high, low = split(unturn(plus[here], minus[here], tw_ref))
-                    results.append(
-                        dot(inner_back_ref[...], jnp.concatenate([high, high, low], 0))
-                    )
-                put(ys, c, rows, group, results[0])
-                put(ys, c + per_device, rows, group, results[1])
-                put(ks.at[s], c, rows, per_device, results[2])
-            return carry
-
-        lax.fori_loop(0, per_device // BATCHED, step, 0, unroll=UNROLL)
+        kernel_copy = peer_copy(kout.at[s], kbuf.at[s], ksend.at[s], krecv.at[s], partner)
+        turned = []
+        for c in range(per_device):
+            for r in (c, c + per_device):
+                x = take(xs, r, rows, group).astype(bf16)
+                turned.append(turn(dot(short, jnp.concatenate([x, x], 0)), tw_ref))
+        specs = [three(jnp.concatenate([t[p] for t in turned], 0), in_ref, p) for p in range(2)]
+
+        def parts_of(p, c):
+            g = specs[p][2 * c * rows : (2 * c + 1) * rows]
+            x = specs[p][(2 * c + 1) * rows : (2 * c + 2) * rows]
+            return g[:, :HALF], g[:, HALF:], x[:, :HALF], x[:, HALF:]
+
+        def to_rows(products, targets):
+            plus_minus = [three(jnp.concatenate(v, 0), inv_ref, p) for p, v in enumerate(products)]
+            plus = plus_minus[0] + plus_minus[1]
+            minus = plus_minus[0] - plus_minus[1]
+            for n, target in enumerate(targets):
+                here = slice(n * rows, (n + 1) * rows)
+                high, low = split(unturn(plus[here], minus[here], tw_ref))
+                put(*target, dot(inner_back_ref[...], jnp.concatenate([high, high, low], 0)))
+
+        products = [[], []]
+        for p in range(2):
+            for c in range(per_device):
+                gr, gi, sr, si = parts_of(p, c)
+                products[p].append(
+                    jnp.concatenate([gr * sr + gi * si, gi * sr - gr * si], 1)
+                )
+        to_rows(products, [(ks.at[s], c, rows, per_device) for c in range(per_device)])
+        for h in range(2):
+            lanes = slice(h * HALF, (h + 1) * HALF)
+            kout[s, :, lanes] = ks[s, h, pl.ds(other, part)].astype(bf16)
+        kernel_copy.start()
+
+        products = [[], []]
+        for p in range(2):
+            for c in range(per_device):
+                gr, gi, sr, si = parts_of(p, c)
+                fr = fspec[s, p, c * rows : (c + 1) * rows, :HALF]
+                fi = fspec[s, p, c * rows : (c + 1) * rows, HALF:]
+                products[p] += [
+                    jnp.concatenate([fr * gr + fi * gi, fr * gi - fi * gr], 1),
+                    jnp.concatenate([fr * sr - fi * si, fr * si + fi * sr], 1),
+                ]
+        to_rows(
+            products,
+            [(ys, r, rows, group) for c in range(per_device) for r in (c, c + per_device)],
+        )
         for h in range(2):
             lanes = slice(h * HALF, (h + 1) * HALF)
             back[s, :, :, lanes] = ys[h].reshape(pieces, group, HALF).astype(bf16)
-            kout[s, :, lanes] = ks[s, h, pl.ds(other, part)].astype(bf16)
         start_exchange(back.at[s], rec.at[s], send_out.at[s], recv_out.at[s])
-        peer_copy(kout.at[s], kbuf.at[s], ksend.at[s], krecv.at[s], partner).start()
 
     stores = []
 
@@ -354,10 +362,6 @@
         all_of(back.at[s], rec.at[s], send_out.at[s], recv_out.at[s]).wait_send()
     for copy in stores:
         copy.wait()
-
-
-UNROLL = 1
-BATCHED = 4
 
 
 def finish_kernel(*refs):
@@ -424,8 +428,8 @@
             dma((segments,)),
             dma((segments,)),
             dma((segments,)),
-            dma,
-            dma,
+            dma((segments,)),
+            dma((segments,)),
             dma((segments,)),
             dma((segments,)),
             dma((len(operands),)),

time: 38.9 us -> 37.2 us (0.956)
  Pallas kernels: 38.1 us -> 36.4 us
    pallas_call x1, Pallas kernels: 36.2 us -> 34.5 us  [on_device(): pl.pallas_call(functools.partial(main_kernel, factor), out_shape=results,...]
where the time goes in v6:
time: 37.2 us; the launch traced here: 37.1 us
  Pallas kernels  36.4 us (98%)
  between operations  0.64 us (2%)
    pallas_call x1, Pallas kernels, on_device(): pl.pallas_call(functools.partial(main_kernel, factor), out_shape=results,...  34.5 us
    pallas_call x1, Pallas kernels, on_device(): pl.pallas_call(finish_kernel, out_shape=results, in_specs=hbm(3), out_spe...  1.88 us

profile of v6, /device:TPU:1, one launch (start us, length us, event | category | flops | bytes accessed | tf_op | source)
XLA Modules:
  0.0 37.1 jit_solution(2295042010953949017)
XLA Ops:
  0.6 34.5 %main.1 = (bf16[256,512]{1,0:T(8,128)(2,1)}, bf16[256,512]{1,0:T(8,128)(2,1)}, f32[2,4,8192]{2,1,0:T(4,128)}) custom-call(bf16[256,512]{1,0:T(8,128)(2,1)} %bitcast.5, bf16[256,512]{1,0:T(8,128)(2,1)} %bitcast.6, bf16[256,512]{1,0:T(8,128)(2,1)} %bitcast.7, f32[2,4,8192]{2,1,0:T(4,128)} %refs_3_.1, bf16[512,512]{1,0:T(8,128)(2,1)} %constant.17.clone.refs_4_, ...), custom_call_target="tpu_custom_call" | custom-call | tf_op jit(solution)/shard_map/main/pallas_call | solution.py:405
  35.2 1.9 %finish.1 = (bf16[256,512]{1,0:T(8,128)(2,1)}, bf16[256,512]{1,0:T(8,128)(2,1)}, f32[2,4,8192]{2,1,0:T(4,128)}) custom-call(bf16[256,512]{1,0:T(8,128)(2,1)} %get-tuple-element.9.refs_0_, bf16[256,512]{1,0:T(8,128)(2,1)} %get-tuple-element.10.refs_1_, f32[2,4,8192]{2,1,0:T(4,128)} %get-tuple-element.11.refs_2_), custom_call_target="tpu_custom_call" | custom-call | tf_op jit(solution)/shard_map/finish/pallas_call | solution.py:443

commit v7 on v6

--- a/solution.py
+++ b/solution.py
@@ -241,13 +241,16 @@
     filter_copies = [
         peer_copy(pf.at[s], pfin.at[s], fsend.at[s], frecv.at[s], partner) for s in range(segments)
     ]
-    for s in range(segments):
+    filter_copies[0].start()
+    start_exchange(pack.at[0], recv.at[0], send_in.at[0], recv_in.at[0])
+    for s in range(1, segments):
         filter_copies[s].start()
-        start_exchange(pack.at[s], recv.at[s], send_in.at[s], recv_in.at[s])
     for n in range(5, 10):
         loads[n].wait()
     for s in range(segments):
         filter_copies[s].wait()
+        if s + 1 < segments:
+            start_exchange(pack.at[s + 1], recv.at[s + 1], send_in.at[s + 1], recv_in.at[s + 1])
         for h in range(2):
             lanes = slice(h * HALF, (h + 1) * HALF)
             fs[s, h, pl.ds(other, part)] = pfin[s, :, lanes].astype(f32)

time: 37.2 us -> 36 us (0.968)
  Pallas kernels: 36.4 us -> 35.2 us
    pallas_call x1, Pallas kernels: 34.5 us -> 33.4 us  [on_device(): pl.pallas_call(functools.partial(main_kernel, factor), out_shape=results,...]
where the time goes in v7:
time: 36 us; the launch traced here: 35.9 us
  Pallas kernels  35.2 us (98%)
  between operations  0.64 us (2%)
    pallas_call x1, Pallas kernels, on_device(): pl.pallas_call(functools.partial(main_kernel, factor), out_shape=results,...  33.4 us
    pallas_call x1, Pallas kernels, on_device(): pl.pallas_call(finish_kernel, out_shape=results, in_specs=hbm(3), out_spe...  1.88 us

profile of v7, /device:TPU:1, one launch (start us, length us, event | category | flops | bytes accessed | tf_op | source)
XLA Modules:
  0.0 35.9 jit_solution(13157835600987597412)
XLA Ops:
  0.6 33.4 %main.1 = (bf16[256,512]{1,0:T(8,128)(2,1)}, bf16[256,512]{1,0:T(8,128)(2,1)}, f32[2,4,8192]{2,1,0:T(4,128)}) custom-call(bf16[256,512]{1,0:T(8,128)(2,1)} %bitcast.5, bf16[256,512]{1,0:T(8,128)(2,1)} %bitcast.6, bf16[256,512]{1,0:T(8,128)(2,1)} %bitcast.7, f32[2,4,8192]{2,1,0:T(4,128)} %refs_3_.1, bf16[512,512]{1,0:T(8,128)(2,1)} %constant.17.clone.refs_4_, ...), custom_call_target="tpu_custom_call" | custom-call | tf_op jit(solution)/shard_map/main/pallas_call | solution.py:408
  34.0 1.9 %finish.1 = (bf16[256,512]{1,0:T(8,128)(2,1)}, bf16[256,512]{1,0:T(8,128)(2,1)}, f32[2,4,8192]{2,1,0:T(4,128)}) custom-call(bf16[256,512]{1,0:T(8,128)(2,1)} %get-tuple-element.9.refs_0_, bf16[256,512]{1,0:T(8,128)(2,1)} %get-tuple-element.10.refs_1_, f32[2,4,8192]{2,1,0:T(4,128)} %get-tuple-element.11.refs_2_), custom_call_target="tpu_custom_call" | custom-call | tf_op jit(solution)/shard_map/finish/pallas_call | solution.py:446

commit v8 on v7

--- a/solution.py
+++ b/solution.py
@@ -247,6 +247,7 @@
         filter_copies[s].start()
     for n in range(5, 10):
         loads[n].wait()
+    short = fwd_ref[:, : 2 * rows]
     for s in range(segments):
         filter_copies[s].wait()
         if s + 1 < segments:
@@ -271,8 +272,6 @@
 
         lax.fori_loop(0, per_device // 2, filter_step, 0)
 
-    short = fwd_ref[:, : 2 * rows]
-    for s in range(segments):
         incoming = all_of(pack.at[s], recv.at[s], send_in.at[s], recv_in.at[s])
         incoming.wait_recv()
         for h in range(2):

time: 36 us -> 35.9 us (level)
  no operation moved by 1% of the time
where the time goes in v8:
time: 35.9 us; the launch traced here: 35.7 us
  Pallas kernels  35.1 us (98%)
  between operations  0.64 us (2%)
    pallas_call x1, Pallas kernels, on_device(): pl.pallas_call(functools.partial(main_kernel, factor), out_shape=results,...  33.2 us
    pallas_call x1, Pallas kernels, on_device(): pl.pallas_call(finish_kernel, out_shape=results, in_specs=hbm(3), out_spe...  1.88 us

profile of v8, /device:TPU:1, one launch (start us, length us, event | category | flops | bytes accessed | tf_op | source)
XLA Modules:
  0.0 35.7 jit_solution(16260773223014929748)
XLA Ops:
  0.6 33.2 %main.1 = (bf16[256,512]{1,0:T(8,128)(2,1)}, bf16[256,512]{1,0:T(8,128)(2,1)}, f32[2,4,8192]{2,1,0:T(4,128)}) custom-call(bf16[256,512]{1,0:T(8,128)(2,1)} %bitcast.5, bf16[256,512]{1,0:T(8,128)(2,1)} %bitcast.6, bf16[256,512]{1,0:T(8,128)(2,1)} %bitcast.7, f32[2,4,8192]{2,1,0:T(4,128)} %refs_3_.1, bf16[512,512]{1,0:T(8,128)(2,1)} %constant.17.clone.refs_4_, ...), custom_call_target="tpu_custom_call" | custom-call | tf_op jit(solution)/shard_map/main/pallas_call | solution.py:407
  33.8 1.9 %finish.1 = (bf16[256,512]{1,0:T(8,128)(2,1)}, bf16[256,512]{1,0:T(8,128)(2,1)}, f32[2,4,8192]{2,1,0:T(4,128)}) custom-call(bf16[256,512]{1,0:T(8,128)(2,1)} %get-tuple-element.9.refs_0_, bf16[256,512]{1,0:T(8,128)(2,1)} %get-tuple-element.10.refs_1_, f32[2,4,8192]{2,1,0:T(4,128)} %get-tuple-element.11.refs_2_), custom_call_target="tpu_custom_call" | custom-call | tf_op jit(solution)/shard_map/finish/pallas_call | solution.py:445

commit v9 on v8

--- a/solution.py
+++ b/solution.py
@@ -216,10 +216,11 @@
         loads[n].start()
     barrier = greet_all()
 
-    loads[3].wait()
     own = dp * part
     other = (1 - dp) * part
-    for s in range(segments):
+    width = pieces * per_device
+
+    def prepare_filter(s):
         for i in range(part // per_device):
             for h in range(2):
                 fs[s, h, pl.ds(own + i * per_device, per_device), :] = filters_ref[
@@ -227,24 +228,29 @@
                 ]
         for h in range(2):
             pf[s, :, h * HALF : (h + 1) * HALF] = fs[s, h, pl.ds(own, part)].astype(bf16)
-    for n in (0, 1, 2, 4):
-        loads[n].wait()
-    width = pieces * per_device
-    for s in range(segments):
+
+    def prepare_blocks(s):
         here = slice(s * width, (s + 1) * width)
         scaled = (grad_ref[:, here].astype(f32) * gate_ref[:, here].astype(f32)).astype(bf16)
         joined = jnp.concatenate([scaled, signal_ref[:, here]], 1)
         moved = dot(perm_ref[...], joined, ((1,), (1,)))
         pack[s] = moved.reshape(pieces, group, tokens).astype(bf16)
 
-    pl.semaphore_wait(barrier, pieces)
     filter_copies = [
         peer_copy(pf.at[s], pfin.at[s], fsend.at[s], frecv.at[s], partner) for s in range(segments)
     ]
+    loads[3].wait()
+    for s in range(segments):
+        prepare_filter(s)
+    for n in (0, 1, 2, 4):
+        loads[n].wait()
+    prepare_blocks(0)
+    pl.semaphore_wait(barrier, pieces)
     filter_copies[0].start()
     start_exchange(pack.at[0], recv.at[0], send_in.at[0], recv_in.at[0])
     for s in range(1, segments):
         filter_copies[s].start()
+        prepare_blocks(s)
     for n in range(5, 10):
         loads[n].wait()
     short = fwd_ref[:, : 2 * rows]

time: 35.9 us -> 35.9 us (level)
  no operation moved by 1% of the time
where the time goes in v9:
time: 35.9 us; the launch traced here: 35.7 us
  Pallas kernels  35.1 us (98%)
  between operations  0.64 us (2%)
    pallas_call x1, Pallas kernels, on_device(): pl.pallas_call(functools.partial(main_kernel, factor), out_shape=results,...  33.2 us
    pallas_call x1, Pallas kernels, on_device(): pl.pallas_call(finish_kernel, out_shape=results, in_specs=hbm(3), out_spe...  1.88 us

profile of v9, /device:TPU:1, one launch (start us, length us, event | category | flops | bytes accessed | tf_op | source)
XLA Modules:
  0.0 35.7 jit_solution(14644240166368114997)
XLA Ops:
  0.6 33.2 %main.1 = (bf16[256,512]{1,0:T(8,128)(2,1)}, bf16[256,512]{1,0:T(8,128)(2,1)}, f32[2,4,8192]{2,1,0:T(4,128)}) custom-call(bf16[256,512]{1,0:T(8,128)(2,1)} %bitcast.5, bf16[256,512]{1,0:T(8,128)(2,1)} %bitcast.6, bf16[256,512]{1,0:T(8,128)(2,1)} %bitcast.7, f32[2,4,8192]{2,1,0:T(4,128)} %refs_3_.1, bf16[512,512]{1,0:T(8,128)(2,1)} %constant.17.clone.refs_4_, ...), custom_call_target="tpu_custom_call" | custom-call | tf_op jit(solution)/shard_map/main/pallas_call | solution.py:413
  33.8 1.9 %finish.1 = (bf16[256,512]{1,0:T(8,128)(2,1)}, bf16[256,512]{1,0:T(8,128)(2,1)}, f32[2,4,8192]{2,1,0:T(4,128)}) custom-call(bf16[256,512]{1,0:T(8,128)(2,1)} %get-tuple-element.9.refs_0_, bf16[256,512]{1,0:T(8,128)(2,1)} %get-tuple-element.10.refs_1_, f32[2,4,8192]{2,1,0:T(4,128)} %get-tuple-element.11.refs_2_), custom_call_target="tpu_custom_call" | custom-call | tf_op jit(solution)/shard_map/finish/pallas_call | solution.py:451
